TPU v7x, 256 devices: a whole 4x4x8 slice. The times are simulated.
256 devices in a mesh: wide: 16 (over y, x), narrow: 16 (over z, core).
Axes of the slice: x: 4, y: 4, z: 8, core: 2. Of those that a mesh axis runs over, the one named last changes fastest.
Arguments:
- vectors: float32 [524288, 128], P(('wide', 'narrow')), may hold values from -24 to 24
- near_blocks: bfloat16 [1024, 3, 512, 512], P(('wide', 'narrow')), may hold values from -0.15625 to 0.15625
- leaf_basis: bfloat16 [524288, 256], P(('wide', 'narrow')), may hold values from -0.125 to 0.125
- transfer: bfloat16 [256, 256, 256], P(('wide', 'narrow')), may hold values from -0.09375 to 0.09375
- leaf_coupling: bfloat16 [256, 6, 256, 256], P(('wide', 'narrow')), may hold values from -0.15625 to 0.15625
- leaf_partners: int32 [256, 6], P(('wide', 'narrow')), may hold values from 0 to 15, as said below
- parent_coupling: bfloat16 [16, 3, 256, 256], P('wide'), may hold values from -0.21875 to 0.21875
- parent_partners: int32 [16, 3], P('wide'), may hold values from 0 to 15, as said below
- shifts: float32 [128], replicated, may hold values from -1 to 1
Outputs:
- filtered: float32 [524288, 128], P(('wide', 'narrow'))
Inputs may be any that keep to these rules, and one draw needn't show every extreme that they name: `leaf_partners`: row l lists 6 different sibling indices, none equal to l mod 16. `parent_partners`: row p lists 3 different parent indices, none equal to p.
All inputs are finite; a program needn't handle non-finite values.
Results may differ from a plain program's by a relative error of at most 0.01.
Values may be sent and summed in bfloat16 or wider, within the bound.
No kernel may reach another device: no remote copies, remote signals or barrier semaphores. Data moves between devices by JAX's collectives and lax.ppermute only.
A program may use at most 64 MiB of HBM per device.

v0:
```python
import functools

import jax
import jax.numpy as jnp
from jax import lax
from jax.experimental import pallas as pl
from jax.experimental.pallas import tpu as pltpu
from jax.sharding import Mesh
from jax.sharding import PartitionSpec as P


BLK = 512
DEGREE = 3
ALL = ("wide_0", "wide_1", "narrow_0", "narrow_1")
NARROW = ("narrow_0", "narrow_1")
WIDE = ("wide_0", "wide_1")
F32 = jnp.float32
BF16 = jnp.bfloat16
VMEM = pl.BlockSpec(memory_space=pltpu.VMEM)
SMEM = pl.BlockSpec(memory_space=pltpu.SMEM)


def cost(flops, moved):
    return pl.CostEstimate(flops=int(flops), bytes_accessed=int(moved), transcendentals=0)


def dot_nn(a, b):
    return lax.dot_general(a, b, (((1,), (0,)), ((), ())), preferred_element_type=F32)


def dot_nt(a, b):
    return lax.dot_general(a, b, (((1,), (1,)), ((), ())), preferred_element_type=F32)


def block(b):
    return slice(b * BLK, (b + 1) * BLK)


def begin_kernel(vec_ref, basis_ref, transfer_ref, v_ref, load_ref, low_ref, high_ref):
    blocks, rank = vec_ref.shape[0] // BLK, basis_ref.shape[1]
    total = None
    for b in range(blocks):
        t = vec_ref[block(b), :]
        v = t.astype(BF16)
        v_ref[block(b), :] = v
        if b == 0:
            low_ref[...] = v
        if b == blocks - 1:
            high_ref[...] = v
        term = dot_nn(t.T.astype(BF16), basis_ref[block(b), :])
        total = term if total is None else total + term
    load_ref[:rank] = transfer_ref[...]
    load_ref[rank:] = total.astype(BF16)


def near_kernel(first, blocks_ref, v_ref, low_ref, high_ref, t_ref, shift_ref, *rest):
    out_ref = rest[-1]
    blocks = blocks_ref.shape[0]
    for b in range(blocks):
        near = dot_nn(blocks_ref[b, 0], low_ref[...] if b == 0 else v_ref[block(b - 1), :])
        near = near + dot_nn(blocks_ref[b, 1], v_ref[block(b), :])
        near = near + dot_nn(blocks_ref[b, 2], high_ref[...] if b == blocks - 1 else v_ref[block(b + 1), :])
        value = near - shift_ref[...] * t_ref[block(b), :]
        if not first:
            value = 2.0 * value - rest[0][block(b), :]
        out_ref[block(b), :] = value


def share_kernel(base, count, *refs):
    matrices, loads, out_ref = refs[:count], refs[count:-1], refs[-1]
    half, rank = out_ref.shape[1:]
    start = pl.multiple_of(base + lax.axis_index("narrow_1") * half, half)
    total = None
    for matrix_ref, load_ref in zip(matrices, loads):
        for slot in range(2):
            term = dot_nn(load_ref[slot, pl.ds(start, half), :], matrix_ref[slot, :rank, :])
            total = term if total is None else total + term
    total = total.astype(BF16)
    for copy in range(out_ref.shape[0]):
        out_ref[copy] = total


def parent_kernel(partner_ref, got_ref, coupling_ref, out_ref):
    total = dot_nt(got_ref[partner_ref[0]], coupling_ref[0])
    for j in range(1, coupling_ref.shape[0]):
        total = total + dot_nt(got_ref[partner_ref[j]], coupling_ref[j])
    out_ref[...] = total.astype(BF16)


def pair_kernel(own_ref, other_ref, out_ref):
    out_ref[0] = own_ref[...]
    out_ref[1] = other_ref[...]


def sibling_kernel(base, count, partner_ref, *refs):
    loads, (coupling_ref, out_ref, held) = refs[:count], refs[count:]
    for k, load_ref in enumerate(loads):
        for slot in range(2):
            held[2 * k + slot] = load_ref[slot, base:, :]
    chips = lax.axis_size("narrow_0")
    chip, core = lax.axis_index("narrow_0"), lax.axis_index("narrow_1")
    half = chips // 2
    total = None
    for j in range(coupling_ref.shape[0]):
        leaf = partner_ref[j]
        parity = lax.rem(leaf, 2)
        away = lax.rem(chip - leaf // 2 + chips, chips)
        own_ring = jnp.logical_or(away == 0, away == half)
        ring_core = jnp.where(own_ring, core, jnp.where(away < half, 0, 1))
        hops = jnp.where(away <= half, away, chips - away)
        at = jnp.where(ring_core == core, hops, half + hops)
        at = 2 * at + jnp.where(parity == ring_core, 0, 1)
        term = dot_nt(held[at], coupling_ref[j])
        total = term if total is None else total + term
    out_ref[...] = total


def far_of(far_ref, mine_ref, theirs_ref, transfer_ref):
    mine, theirs = dot_nt(mine_ref[...], transfer_ref[...]), dot_nt(theirs_ref[...], transfer_ref[...])
    first = lax.axis_index("narrow_1") == 0
    down = jnp.concatenate([jnp.where(first, mine, theirs), jnp.where(first, theirs, mine)], axis=0)
    return (far_ref[...] + down).T.astype(BF16)


def step_kernel(
    scale, part_ref, far_ref, mine_ref, theirs_ref, transfer_ref, basis_ref, t_ref, v_ref, load_ref, low_ref, high_ref
):
    blocks = part_ref.shape[0] // BLK
    far = far_of(far_ref, mine_ref, theirs_ref, transfer_ref)
    total = None
    for b in range(blocks):
        basis = basis_ref[block(b), :]
        t = part_ref[block(b), :] + scale * dot_nn(basis, far)
        t_ref[block(b), :] = t
        v = t.astype(BF16)
        v_ref[block(b), :] = v
        if b == 0:
            low_ref[...] = v
        if b == blocks - 1:
            high_ref[...] = v
        term = dot_nn(t.T.astype(BF16), basis)
        total = term if total is None else total + term
    load_ref[...] = total.astype(BF16)


def final_kernel(scale, part_ref, far_ref, mine_ref, theirs_ref, transfer_ref, basis_ref, out_ref, squares_ref):
    far = far_of(far_ref, mine_ref, theirs_ref, transfer_ref)
    total = None
    for b in range(part_ref.shape[0] // BLK):
        t = part_ref[block(b), :] + scale * dot_nn(basis_ref[block(b), :], far)
        out_ref[block(b), :] = t
        term = jnp.sum((t * t).reshape(BLK // 8, 8, t.shape[1]), axis=0)
        total = term if total is None else total + term
    for copy in range(squares_ref.shape[0]):
        squares_ref[copy] = total


def gather_kernel(got_ref, out_ref):
    total = jnp.sum(got_ref[...], axis=0)
    for copy in range(out_ref.shape[0]):
        out_ref[copy] = total


def scale_kernel(total_rows, t_ref, got_ref, out_ref):
    squares = jnp.sum(jnp.sum(got_ref[...], axis=0), axis=0, keepdims=True)
    out_ref[...] = t_ref[...] / jnp.sqrt(squares / total_rows + 1e-06)


def call(kernel, outs, operands, specs=None, flops=1e6, moved=1e6, scratch=()):
    return pl.pallas_call(
        kernel,
        out_shape=[jax.ShapeDtypeStruct(s, d) for s, d in outs],
        in_specs=specs or [VMEM] * len(operands),
        out_specs=[VMEM] * len(outs),
        scratch_shapes=scratch,
        compiler_params=pltpu.CompilerParams(vmem_limit_bytes=16 * 1024 * 1024),
        cost_estimate=cost(flops, moved),
    )(*operands)


def exchanged(pieces, axes):
    return lax.all_to_all(pieces, axes, split_axis=0, concat_axis=0, tiled=True)


def shards(vectors, near_blocks, leaf_basis, transfer, leaf_coupling, leaf_partners, parent_coupling, parent_partners, shifts):
    rows, cols = vectors.shape
    rank = leaf_basis.shape[1]
    blocks = near_blocks.shape[0]
    n_narrow, n_wide = lax.axis_size(NARROW), lax.axis_size(WIDE)
    chips = lax.axis_size("narrow_0")
    devices = n_narrow * n_wide
    half = cols // 2
    matrix = transfer[0]
    shift = shifts[None, :]
    up = [(i, i + 1) for i in range(devices - 1)]
    down = [(b, a) for a, b in up]
    swap = [(0, 1), (1, 0)]
    count = chips

    def state(size):
        return [((rows, cols), BF16), ((size, rank), BF16), ((BLK, cols), BF16), ((BLK, cols), BF16)]

    leaf_flops = 2 * 2 * rows * rank * cols

    away = [(2 * c, 2 * ((c + 1) % chips)) for c in range(chips)]
    away += [(2 * c + 1, 2 * ((c - 1) % chips) + 1) for c in range(chips)]

    previous, t = None, vectors
    v, load, low, high = call(begin_kernel, state(rank + cols), (vectors, leaf_basis, matrix), flops=leaf_flops)
    matrices = None
    for step in range(DEGREE):
        scale = 1.0 if step == 0 else 2.0
        base = rank if step == 0 else 0
        partner = lax.ppermute(load, "narrow_1", swap)
        (pair,) = call(pair_kernel, [((2, *load.shape), BF16)], (load, partner))
        ring, crossed = [pair], []
        for s in range(1, chips // 2 + 1):
            ring.append(lax.ppermute(ring[-1], NARROW, away))
            if s < chips // 2:
                crossed.append(lax.ppermute(ring[-1], "narrow_1", swap))
        loads = ring + crossed
        matrices = loads if matrices is None else matrices
        low_in = lax.ppermute(high, ALL, up)
        high_in = lax.ppermute(low, ALL, down)
        operands = [near_blocks, v, low_in, high_in, t, shift] + ([] if previous is None else [previous])
        (value,) = call(
            functools.partial(near_kernel, previous is None),
            [((rows, cols), F32)],
            operands,
            flops=2 * 3 * blocks * BLK * BLK * cols,
        )
        (share,) = call(
            functools.partial(share_kernel, base, count),
            [((n_wide, half, rank), BF16)],
            matrices + loads,
            flops=2 * n_narrow * half * rank * rank,
        )
        (far,) = call(
            functools.partial(sibling_kernel, base, count),
            [((cols, rank), F32)],
            (leaf_partners[0], *loads, leaf_coupling[0]),
            [SMEM] + [VMEM] * (count + 1),
            flops=6 * 2 * rank * rank * cols,
            scratch=[pltpu.VMEM((2 * count, cols, rank), BF16)],
        )
        gathered = exchanged(share, WIDE)
        (mine,) = call(
            parent_kernel,
            [((half, rank), BF16)],
            (parent_partners[0], gathered, parent_coupling[0]),
            [SMEM, VMEM, VMEM],
        )
        theirs = lax.ppermute(mine, "narrow_1", swap)
        operands = (value, far, mine, theirs, matrix, leaf_basis)
        previous = t
        if step < DEGREE - 1:
            t, v, load, low, high = call(
                functools.partial(step_kernel, scale),
                [((rows, cols), F32)] + state(cols),
                operands,
                flops=2 * leaf_flops,
            )
        else:
            out, squares = call(
                functools.partial(final_kernel, scale),
                [((rows, cols), F32), ((n_narrow, 8, cols), F32)],
                operands,
                flops=leaf_flops,
            )
    squares = exchanged(squares, NARROW)
    (squares,) = call(gather_kernel, [((n_wide, 8, cols), F32)], (squares,))
    squares = exchanged(squares, WIDE)
    (out,) = call(functools.partial(scale_kernel, rows * devices), [((rows, cols), F32)], (out, squares))
    return out


def solution(mesh):
    finer = Mesh(mesh.devices.reshape(4, 4, 8, 2), ALL)
    placed = (
        P(ALL, None),
        P(ALL, None, None, None),
        P(ALL, None),
        P(ALL, None, None),
        P(ALL, None, None, None),
        P(ALL, None),
        P(WIDE, None, None, None),
        P(WIDE, None),
        P(),
    )
    return jax.shard_map(shards, mesh=finer, in_specs=placed, out_specs=P(ALL, None), check_vma=False)
```

profile of v0, /device:TPU:1, one launch (start us, length us, event | category | flops | bytes accessed | tf_op | source)
XLA Modules:
  0.0 239.8 jit_solution(9152798510587730431)
XLA Ops:
  4.6 3.2 %collective-permute-start.2 = (bf16[384,256]{1,0:T(8,128)(2,1)S(1)}, bf16[384,256]{1,0:T(8,128)(2,1)S(1)}, u32[]{:S(2)}, u32[]{:S(2)}) collective-permute-start(bf16[384,256]{1,0:T(8,128)(2,1)S(1)} %get-tuple-element.24.own_ref), channel_id=1, source_target_pairs={{0,1},{1,0},{2,3},{3,2},{4,5},{5,4},{6,7},{7,6},{8,9},{9,8},{10,11... | collective-permute-start | bytes 589832 | tf_op jit(solution)/shard_map/ppermute | solution.py:214
  8.9 3.9 %collective-permute-start.3 = (bf16[2,384,256]{2,1,0:T(8,128)(2,1)S(1)}, bf16[2,384,256]{2,1,0:T(8,128)(2,1)S(1)}, u32[]{:S(2)}, u32[]{:S(2)}) collective-permute-start(bf16[2,384,256]{2,1,0:T(8,128)(2,1)S(1)} %shard_map.93.refs_0_.refs_8_), channel_id=1, source_target_pairs={{0,2},{2,4},{4,6},{6,8},{8,10},{10,12},{12,14},{14,0},{1,15},{3,1}... | collective-permute-start | bytes 1179656 | tf_op jit(solution)/shard_map/ppermute | solution.py:218
  12.8 4.7 %collective-permute-done.3.refs_1_.refs_9_ = bf16[2,384,256]{2,1,0:T(8,128)(2,1)S(1)} collective-permute-done((bf16[2,384,256]{2,1,0:T(8,128)(2,1)S(1)}, bf16[2,384,256]{2,1,0:T(8,128)(2,1)S(1)}, u32[]{:S(2)}, u32[]{:S(2)}) %collective-permute-start.3) | collective-permute-done | bytes 393248 | tf_op jit(solution)/shard_map/ppermute | solution.py:218
  17.5 3.1 %collective-permute-start.4 = (bf16[2,384,256]{2,1,0:T(8,128)(2,1)S(1)}, bf16[2,384,256]{2,1,0:T(8,128)(2,1)S(1)}, u32[]{:S(2)}, u32[]{:S(2)}) collective-permute-start(bf16[2,384,256]{2,1,0:T(8,128)(2,1)S(1)} %collective-permute-done.3.refs_1_.refs_9_), channel_id=1, source_target_pairs={{0,2},{2,4},{4,6},{6,8},{8,10},{10,12},{12,14},{14,0},{1,15},{3,1}... | collective-permute-start | bytes 1179656 | tf_op jit(solution)/shard_map/ppermute | solution.py:218
  20.6 4.7 %collective-permute-done.4.refs_2_.refs_10_ = bf16[2,384,256]{2,1,0:T(8,128)(2,1)S(1)} collective-permute-done((bf16[2,384,256]{2,1,0:T(8,128)(2,1)S(1)}, bf16[2,384,256]{2,1,0:T(8,128)(2,1)S(1)}, u32[]{:S(2)}, u32[]{:S(2)}) %collective-permute-start.4) | collective-permute-done | bytes 393248 | tf_op jit(solution)/shard_map/ppermute | solution.py:218
  25.4 3.1 %collective-permute-start.5 = (bf16[2,384,256]{2,1,0:T(8,128)(2,1)S(1)}, bf16[2,384,256]{2,1,0:T(8,128)(2,1)S(1)}, u32[]{:S(2)}, u32[]{:S(2)}) collective-permute-start(bf16[2,384,256]{2,1,0:T(8,128)(2,1)S(1)} %collective-permute-done.4.refs_2_.refs_10_), channel_id=1, source_target_pairs={{0,2},{2,4},{4,6},{6,8},{8,10},{10,12},{12,14},{14,0},{1,15},{3,1}... | collective-permute-start | bytes 1179656 | tf_op jit(solution)/shard_map/ppermute | solution.py:218
  29.0 4.2 %collective-permute-done.5.refs_3_.refs_11_ = bf16[2,384,256]{2,1,0:T(8,128)(2,1)S(1)} collective-permute-done((bf16[2,384,256]{2,1,0:T(8,128)(2,1)S(1)}, bf16[2,384,256]{2,1,0:T(8,128)(2,1)S(1)}, u32[]{:S(2)}, u32[]{:S(2)}) %collective-permute-start.5) | collective-permute-done | bytes 393248 | tf_op jit(solution)/shard_map/ppermute | solution.py:218
  33.2 3.1 %collective-permute-start.6 = (bf16[2,384,256]{2,1,0:T(8,128)(2,1)S(1)}, bf16[2,384,256]{2,1,0:T(8,128)(2,1)S(1)}, u32[]{:S(2)}, u32[]{:S(2)}) collective-permute-start(bf16[2,384,256]{2,1,0:T(8,128)(2,1)S(1)} %collective-permute-done.5.refs_3_.refs_11_), channel_id=1, source_target_pairs={{0,2},{2,4},{4,6},{6,8},{8,10},{10,12},{12,14},{14,0},{1,15},{3,1}... | collective-permute-start | bytes 1179656 | tf_op jit(solution)/shard_map/ppermute | solution.py:218
  37.3 3.8 %collective-permute-done.6.refs_4_.refs_12_ = bf16[2,384,256]{2,1,0:T(8,128)(2,1)S(1)} collective-permute-done((bf16[2,384,256]{2,1,0:T(8,128)(2,1)S(1)}, bf16[2,384,256]{2,1,0:T(8,128)(2,1)S(1)}, u32[]{:S(2)}, u32[]{:S(2)}) %collective-permute-start.6) | collective-permute-done | bytes 393248 | tf_op jit(solution)/shard_map/ppermute | solution.py:218
  43.8 6.9 %all-to-all-start = ((bf16[16,64,256]{2,1,0:T(8,128)(2,1)}), bf16[16,64,256]{2,1,0:T(8,128)(2,1)S(1)}, u32[]{:S(2)}, u32[]{:S(2)}) async-start(bf16[16,64,256]{2,1,0:T(8,128)(2,1)} %copy-done.27), calls=%async_computation | async-start | bytes 1048576 | tf_op jit(solution)/shard_map/all_to_all | solution.py:182
  50.7 5.7 %collective-permute-start = (bf16[512,128]{1,0:T(8,128)(2,1)}, bf16[512,128]{1,0:T(8,128)(2,1)S(1)}, u32[]{:S(2)}, u32[]{:S(2)}) collective-permute-start(bf16[512,128]{1,0:T(8,128)(2,1)} %copy-done.82), channel_id=1, source_target_pairs={{0,1},{1,2},{2,3},{3,4},{4,5},{5,6},{6,7},{7,8},{8,9},{9,10},{10,1... | collective-permute-start | bytes 393224 | tf_op jit(solution)/shard_map/ppermute | solution.py:223
  56.5 2.9 %collective-permute-start.1 = (bf16[512,128]{1,0:T(8,128)(2,1)}, bf16[512,128]{1,0:T(8,128)(2,1)}, u32[]{:S(2)}, u32[]{:S(2)}) collective-permute-start(bf16[512,128]{1,0:T(8,128)(2,1)} %copy-done.81), channel_id=1, source_target_pairs={{1,0},{2,1},{3,2},{4,3},{5,4},{6,5},{7,6},{8,7},{9,8},{10,9},{11,1... | collective-permute-start | bytes 393224 | tf_op jit(solution)/shard_map/ppermute | solution.py:224
  60.6 6.7 %collective-permute-start.10 = (bf16[64,256]{1,0:T(8,128)(2,1)S(1)}, bf16[64,256]{1,0:T(8,128)(2,1)S(1)}, u32[]{:S(2)}, u32[]{:S(2)}) collective-permute-start(bf16[64,256]{1,0:T(8,128)(2,1)S(1)} %shard_map.96.mine_ref), channel_id=1, source_target_pairs={{0,1},{1,0},{2,3},{3,2},{4,5},{5,4},{6,7},{7,6},{8,9},{9,8},{10,11... | collective-permute-start | bytes 98312 | tf_op jit(solution)/shard_map/ppermute | solution.py:253
  67.9 2.8 %copy-done = bf16[4,3,512,512]{3,2,1,0:T(8,128)(2,1)S(1)} copy-done((bf16[4,3,512,512]{3,2,1,0:T(8,128)(2,1)S(1)}, bf16[4,3,512,512]{3,2,1,0:T(8,128)(2,1)}, u32[]{:S(2)}) %copy-start) | copy-done | bytes 6291480
  82.9 2.9 %collective-permute-start.14 = (bf16[2,128,256]{2,1,0:T(8,128)(2,1)S(1)}, bf16[2,128,256]{2,1,0:T(8,128)(2,1)S(1)}, u32[]{:S(2)}, u32[]{:S(2)}) collective-permute-start(bf16[2,128,256]{2,1,0:T(8,128)(2,1)S(1)} %shard_map.99.refs_0_.refs_8_), channel_id=1, source_target_pairs={{0,2},{2,4},{4,6},{6,8},{8,10},{10,12},{12,14},{14,0},{1,15},{3,1}... | collective-permute-start | bytes 393224 | tf_op jit(solution)/shard_map/ppermute | solution.py:218
  87.7 3.1 %collective-permute-start.15 = (bf16[2,128,256]{2,1,0:T(8,128)(2,1)S(1)}, bf16[2,128,256]{2,1,0:T(8,128)(2,1)S(1)}, u32[]{:S(2)}, u32[]{:S(2)}) collective-permute-start(bf16[2,128,256]{2,1,0:T(8,128)(2,1)S(1)} %collective-permute-done.14.refs_1_.refs_9_), channel_id=1, source_target_pairs={{0,2},{2,4},{4,6},{6,8},{8,10},{10,12},{12,14},{14,0},{1,15},{3,1}... | collective-permute-start | bytes 393224 | tf_op jit(solution)/shard_map/ppermute | solution.py:218
  92.8 3.1 %collective-permute-start.16 = (bf16[2,128,256]{2,1,0:T(8,128)(2,1)S(1)}, bf16[2,128,256]{2,1,0:T(8,128)(2,1)S(1)}, u32[]{:S(2)}, u32[]{:S(2)}) collective-permute-start(bf16[2,128,256]{2,1,0:T(8,128)(2,1)S(1)} %collective-permute-done.15.refs_2_.refs_10_), channel_id=1, source_target_pairs={{0,2},{2,4},{4,6},{6,8},{8,10},{10,12},{12,14},{14,0},{1,15},{3,1}... | collective-permute-start | bytes 393224 | tf_op jit(solution)/shard_map/ppermute | solution.py:218
  97.8 3.1 %collective-permute-start.17 = (bf16[2,128,256]{2,1,0:T(8,128)(2,1)S(1)}, bf16[2,128,256]{2,1,0:T(8,128)(2,1)S(1)}, u32[]{:S(2)}, u32[]{:S(2)}) collective-permute-start(bf16[2,128,256]{2,1,0:T(8,128)(2,1)S(1)} %collective-permute-done.16.refs_3_.refs_11_), channel_id=1, source_target_pairs={{0,2},{2,4},{4,6},{6,8},{8,10},{10,12},{12,14},{14,0},{1,15},{3,1}... | collective-permute-start | bytes 393224 | tf_op jit(solution)/shard_map/ppermute | solution.py:218
  109.4 8.0 %all-to-all-start.1 = ((bf16[16,64,256]{2,1,0:T(8,128)(2,1)}), bf16[16,64,256]{2,1,0:T(8,128)(2,1)}, u32[]{:S(2)}, u32[]{:S(2)}) async-start(bf16[16,64,256]{2,1,0:T(8,128)(2,1)} %copy-done.26), calls=%async_computation.1 | async-start | bytes 1048576 | tf_op jit(solution)/shard_map/all_to_all | solution.py:182
  117.4 5.5 %collective-permute-start.11 = (bf16[512,128]{1,0:T(8,128)(2,1)}, bf16[512,128]{1,0:T(8,128)(2,1)}, u32[]{:S(2)}, u32[]{:S(2)}) collective-permute-start(bf16[512,128]{1,0:T(8,128)(2,1)} %copy-done.80), channel_id=1, source_target_pairs={{0,1},{1,2},{2,3},{3,4},{4,5},{5,6},{6,7},{7,8},{8,9},{9,10},{10,1... | collective-permute-start | bytes 393224 | tf_op jit(solution)/shard_map/ppermute | solution.py:223
  122.9 3.5 %collective-permute-start.12 = (bf16[512,128]{1,0:T(8,128)(2,1)}, bf16[512,128]{1,0:T(8,128)(2,1)}, u32[]{:S(2)}, u32[]{:S(2)}) collective-permute-start(bf16[512,128]{1,0:T(8,128)(2,1)} %copy-done.79), channel_id=1, source_target_pairs={{1,0},{2,1},{3,2},{4,3},{5,4},{6,5},{7,6},{8,7},{9,8},{10,9},{11,1... | collective-permute-start | bytes 393224 | tf_op jit(solution)/shard_map/ppermute | solution.py:224
  128.8 6.4 %collective-permute-start.21 = (bf16[64,256]{1,0:T(8,128)(2,1)S(1)}, bf16[64,256]{1,0:T(8,128)(2,1)S(1)}, u32[]{:S(2)}, u32[]{:S(2)}) collective-permute-start(bf16[64,256]{1,0:T(8,128)(2,1)S(1)} %shard_map.102.mine_ref), channel_id=1, source_target_pairs={{0,1},{1,0},{2,3},{3,2},{4,5},{5,4},{6,7},{7,6},{8,9},{9,8},{10,11... | collective-permute-start | bytes 98312 | tf_op jit(solution)/shard_map/ppermute | solution.py:253
  141.6 2.9 %shard_map.98.part_ref = f32[2048,128]{1,0:T(8,128)S(1)} custom-call(bf16[4,3,512,512]{3,2,1,0:T(8,128)(2,1)S(1)} %copy-done.1, bf16[2048,128]{1,0:T(8,128)(2,1)S(1)} %copy-done.37, bf16[512,128]{1,0:T(8,128)(2,1)} %collective-permute-done.11.low_ref, bf16[512,128]{1,0:T(8,128)(2,1)} %collective-permute-done.12.high_ref, f32[2048,128]{1,0:T(8,128)S(1)} %copy-done.18, ...), custom_call_target="tpu_custom_call" | custom-call | flops 805306368 | bytes 1000000 | tf_op jit(solution)/shard_map/pallas_call | solution.py:170
  153.6 3.0 %collective-permute-start.26 = (bf16[2,128,256]{2,1,0:T(8,128)(2,1)S(1)}, bf16[2,128,256]{2,1,0:T(8,128)(2,1)S(1)}, u32[]{:S(2)}, u32[]{:S(2)}) collective-permute-start(bf16[2,128,256]{2,1,0:T(8,128)(2,1)S(1)} %collective-permute-done.25.refs_1_.refs_9_), channel_id=1, source_target_pairs={{0,2},{2,4},{4,6},{6,8},{8,10},{10,12},{12,14},{14,0},{1,15},{3,1}... | collective-permute-start | bytes 393224 | tf_op jit(solution)/shard_map/ppermute | solution.py:218
  158.5 3.1 %collective-permute-start.27 = (bf16[2,128,256]{2,1,0:T(8,128)(2,1)S(1)}, bf16[2,128,256]{2,1,0:T(8,128)(2,1)S(1)}, u32[]{:S(2)}, u32[]{:S(2)}) collective-permute-start(bf16[2,128,256]{2,1,0:T(8,128)(2,1)S(1)} %collective-permute-done.26.refs_2_.refs_10_), channel_id=1, source_target_pairs={{0,2},{2,4},{4,6},{6,8},{8,10},{10,12},{12,14},{14,0},{1,15},{3,1}... | collective-permute-start | bytes 393224 | tf_op jit(solution)/shard_map/ppermute | solution.py:218
  163.5 3.1 %collective-permute-start.28 = (bf16[2,128,256]{2,1,0:T(8,128)(2,1)S(1)}, bf16[2,128,256]{2,1,0:T(8,128)(2,1)S(1)}, u32[]{:S(2)}, u32[]{:S(2)}) collective-permute-start(bf16[2,128,256]{2,1,0:T(8,128)(2,1)S(1)} %collective-permute-done.27.refs_3_.refs_11_), channel_id=1, source_target_pairs={{0,2},{2,4},{4,6},{6,8},{8,10},{10,12},{12,14},{14,0},{1,15},{3,1}... | collective-permute-start | bytes 393224 | tf_op jit(solution)/shard_map/ppermute | solution.py:218
  175.9 7.3 %all-to-all-start.2 = ((bf16[16,64,256]{2,1,0:T(8,128)(2,1)}), bf16[16,64,256]{2,1,0:T(8,128)(2,1)S(1)}, u32[]{:S(2)}, u32[]{:S(2)}) async-start(bf16[16,64,256]{2,1,0:T(8,128)(2,1)} %copy-done.25), calls=%async_computation.2 | async-start | bytes 1048576 | tf_op jit(solution)/shard_map/all_to_all | solution.py:182
  183.2 5.5 %collective-permute-start.22 = (bf16[512,128]{1,0:T(8,128)(2,1)}, bf16[512,128]{1,0:T(8,128)(2,1)S(1)}, u32[]{:S(2)}, u32[]{:S(2)}) collective-permute-start(bf16[512,128]{1,0:T(8,128)(2,1)} %copy-done.78), channel_id=1, source_target_pairs={{0,1},{1,2},{2,3},{3,4},{4,5},{5,6},{6,7},{7,8},{8,9},{9,10},{10,1... | collective-permute-start | bytes 393224 | tf_op jit(solution)/shard_map/ppermute | solution.py:223
  188.7 2.9 %collective-permute-start.23 = (bf16[512,128]{1,0:T(8,128)(2,1)}, bf16[512,128]{1,0:T(8,128)(2,1)S(1)}, u32[]{:S(2)}, u32[]{:S(2)}) collective-permute-start(bf16[512,128]{1,0:T(8,128)(2,1)} %copy-done.77), channel_id=1, source_target_pairs={{1,0},{2,1},{3,2},{4,3},{5,4},{6,5},{7,6},{8,7},{9,8},{10,9},{11,1... | collective-permute-start | bytes 393224 | tf_op jit(solution)/shard_map/ppermute | solution.py:224
  194.1 6.6 %collective-permute-start.32 = (bf16[64,256]{1,0:T(8,128)(2,1)S(1)}, bf16[64,256]{1,0:T(8,128)(2,1)S(1)}, u32[]{:S(2)}, u32[]{:S(2)}) collective-permute-start(bf16[64,256]{1,0:T(8,128)(2,1)S(1)} %shard_map.108.mine_ref), channel_id=1, source_target_pairs={{0,1},{1,0},{2,3},{3,2},{4,5},{5,4},{6,7},{7,6},{8,9},{9,8},{10,11... | collective-permute-start | bytes 98312 | tf_op jit(solution)/shard_map/ppermute | solution.py:253
  213.7 10.7 %all_to_all.25.got_ref = f32[16,8,128]{2,1,0:T(8,128)S(1)} all-to-all(f32[16,8,128]{2,1,0:T(8,128)S(1)} %get-tuple-element.36), channel_id=1, replica_groups=mesh['wide_0'=4,'wide_1'=4,'narrow_0'=8,'narrow_1'=2] {'narrow_0','narro..., dimensions={0} | all-to-all | bytes 131072 | tf_op jit(solution)/shard_map/all_to_all | solution.py:182
  224.4 14.3 %all_to_all.26.got_ref = f32[16,8,128]{2,1,0:T(8,128)S(1)} all-to-all(f32[16,8,128]{2,1,0:T(8,128)S(1)} %shard_map.110), channel_id=1, replica_groups=mesh['wide_0'=4,'wide_1'=4,'narrow_0'=8,'narrow_1'=2] {'wide_0','wide_1'}, dimensions={0} | all-to-all | bytes 131072 | tf_op jit(solution)/shard_map/all_to_all | solution.py:182
  (229 shorter events, 85.3 us)
Async XLA Ops:
  4.6 4.3 %collective-permute-start.2 = (bf16[384,256]{1,0:T(8,128)(2,1)S(1)}, bf16[384,256]{1,0:T(8,128)(2,1)S(1)}, u32[]{:S(2)}, u32[]{:S(2)}) collective-permute-start(bf16[384,256]{1,0:T(8,128)(2,1)S(1)} %get-tuple-element.24.own_ref), channel_id=1, source_target_pairs={{0,1},{1,0},{2,3},{3,2},{4,5},{5,4},{6,7},{7,6},{8,9},{9,8},{10,11... | collective-permute-start | bytes 589832 | tf_op jit(solution)/shard_map/ppermute | solution.py:214
  8.9 8.7 %collective-permute-start.3 = (bf16[2,384,256]{2,1,0:T(8,128)(2,1)S(1)}, bf16[2,384,256]{2,1,0:T(8,128)(2,1)S(1)}, u32[]{:S(2)}, u32[]{:S(2)}) collective-permute-start(bf16[2,384,256]{2,1,0:T(8,128)(2,1)S(1)} %shard_map.93.refs_0_.refs_8_), channel_id=1, source_target_pairs={{0,2},{2,4},{4,6},{6,8},{8,10},{10,12},{12,14},{14,0},{1,15},{3,1}... | collective-permute-start | bytes 1179656 | tf_op jit(solution)/shard_map/ppermute | solution.py:218
  17.5 7.8 %collective-permute-start.4 = (bf16[2,384,256]{2,1,0:T(8,128)(2,1)S(1)}, bf16[2,384,256]{2,1,0:T(8,128)(2,1)S(1)}, u32[]{:S(2)}, u32[]{:S(2)}) collective-permute-start(bf16[2,384,256]{2,1,0:T(8,128)(2,1)S(1)} %collective-permute-done.3.refs_1_.refs_9_), channel_id=1, source_target_pairs={{0,2},{2,4},{4,6},{6,8},{8,10},{10,12},{12,14},{14,0},{1,15},{3,1}... | collective-permute-start | bytes 1179656 | tf_op jit(solution)/shard_map/ppermute | solution.py:218
  25.4 7.8 %collective-permute-start.5 = (bf16[2,384,256]{2,1,0:T(8,128)(2,1)S(1)}, bf16[2,384,256]{2,1,0:T(8,128)(2,1)S(1)}, u32[]{:S(2)}, u32[]{:S(2)}) collective-permute-start(bf16[2,384,256]{2,1,0:T(8,128)(2,1)S(1)} %collective-permute-done.4.refs_2_.refs_10_), channel_id=1, source_target_pairs={{0,2},{2,4},{4,6},{6,8},{8,10},{10,12},{12,14},{14,0},{1,15},{3,1}... | collective-permute-start | bytes 1179656 | tf_op jit(solution)/shard_map/ppermute | solution.py:218
  28.5 8.8 %collective-permute-start.7 = (bf16[2,384,256]{2,1,0:T(8,128)(2,1)S(1)}, bf16[2,384,256]{2,1,0:T(8,128)(2,1)S(1)}, u32[]{:S(2)}, u32[]{:S(2)}) collective-permute-start(bf16[2,384,256]{2,1,0:T(8,128)(2,1)S(1)} %collective-permute-done.3.refs_1_.refs_9_), channel_id=1, source_target_pairs={{0,1},{1,0},{2,3},{3,2},{4,5},{5,4},{6,7},{7,6},{8,9},{9,8},{10,11... | collective-permute-start | bytes 1179656 | tf_op jit(solution)/shard_map/ppermute | solution.py:220
  28.5 8.8 %collective-permute-start.8 = (bf16[2,384,256]{2,1,0:T(8,128)(2,1)S(1)}, bf16[2,384,256]{2,1,0:T(8,128)(2,1)S(1)}, u32[]{:S(2)}, u32[]{:S(2)}) collective-permute-start(bf16[2,384,256]{2,1,0:T(8,128)(2,1)S(1)} %collective-permute-done.4.refs_2_.refs_10_), channel_id=1, source_target_pairs={{0,1},{1,0},{2,3},{3,2},{4,5},{5,4},{6,7},{7,6},{8,9},{9,8},{10,11... | collective-permute-start | bytes 1179656 | tf_op jit(solution)/shard_map/ppermute | solution.py:220
  33.2 7.8 %collective-permute-start.6 = (bf16[2,384,256]{2,1,0:T(8,128)(2,1)S(1)}, bf16[2,384,256]{2,1,0:T(8,128)(2,1)S(1)}, u32[]{:S(2)}, u32[]{:S(2)}) collective-permute-start(bf16[2,384,256]{2,1,0:T(8,128)(2,1)S(1)} %collective-permute-done.5.refs_3_.refs_11_), channel_id=1, source_target_pairs={{0,2},{2,4},{4,6},{6,8},{8,10},{10,12},{12,14},{14,0},{1,15},{3,1}... | collective-permute-start | bytes 1179656 | tf_op jit(solution)/shard_map/ppermute | solution.py:218
  36.3 4.7 %collective-permute-start.9 = (bf16[2,384,256]{2,1,0:T(8,128)(2,1)S(1)}, bf16[2,384,256]{2,1,0:T(8,128)(2,1)S(1)}, u32[]{:S(2)}, u32[]{:S(2)}) collective-permute-start(bf16[2,384,256]{2,1,0:T(8,128)(2,1)S(1)} %collective-permute-done.5.refs_3_.refs_11_), channel_id=1, source_target_pairs={{0,1},{1,0},{2,3},{3,2},{4,5},{5,4},{6,7},{7,6},{8,9},{9,8},{10,11... | collective-permute-start | bytes 1179656 | tf_op jit(solution)/shard_map/ppermute | solution.py:220
  43.8 15.9 %all-to-all-start = ((bf16[16,64,256]{2,1,0:T(8,128)(2,1)}), bf16[16,64,256]{2,1,0:T(8,128)(2,1)S(1)}, u32[]{:S(2)}, u32[]{:S(2)}) async-start(bf16[16,64,256]{2,1,0:T(8,128)(2,1)} %copy-done.27), calls=%async_computation | async-start | bytes 1048576 | tf_op jit(solution)/shard_map/all_to_all | solution.py:182
  50.7 16.5 %collective-permute-start = (bf16[512,128]{1,0:T(8,128)(2,1)}, bf16[512,128]{1,0:T(8,128)(2,1)S(1)}, u32[]{:S(2)}, u32[]{:S(2)}) collective-permute-start(bf16[512,128]{1,0:T(8,128)(2,1)} %copy-done.82), channel_id=1, source_target_pairs={{0,1},{1,2},{2,3},{3,4},{4,5},{5,6},{6,7},{7,8},{8,9},{9,10},{10,1... | collective-permute-start | bytes 393224 | tf_op jit(solution)/shard_map/ppermute | solution.py:223
  56.5 11.4 %collective-permute-start.1 = (bf16[512,128]{1,0:T(8,128)(2,1)}, bf16[512,128]{1,0:T(8,128)(2,1)}, u32[]{:S(2)}, u32[]{:S(2)}) collective-permute-start(bf16[512,128]{1,0:T(8,128)(2,1)} %copy-done.81), channel_id=1, source_target_pairs={{1,0},{2,1},{3,2},{4,3},{5,4},{6,5},{7,6},{8,7},{9,8},{10,9},{11,1... | collective-permute-start | bytes 393224 | tf_op jit(solution)/shard_map/ppermute | solution.py:224
  60.6 18.2 %collective-permute-start.10 = (bf16[64,256]{1,0:T(8,128)(2,1)S(1)}, bf16[64,256]{1,0:T(8,128)(2,1)S(1)}, u32[]{:S(2)}, u32[]{:S(2)}) collective-permute-start(bf16[64,256]{1,0:T(8,128)(2,1)S(1)} %shard_map.96.mine_ref), channel_id=1, source_target_pairs={{0,1},{1,0},{2,3},{3,2},{4,5},{5,4},{6,7},{7,6},{8,9},{9,8},{10,11... | collective-permute-start | bytes 98312 | tf_op jit(solution)/shard_map/ppermute | solution.py:253
  82.9 4.9 %collective-permute-start.14 = (bf16[2,128,256]{2,1,0:T(8,128)(2,1)S(1)}, bf16[2,128,256]{2,1,0:T(8,128)(2,1)S(1)}, u32[]{:S(2)}, u32[]{:S(2)}) collective-permute-start(bf16[2,128,256]{2,1,0:T(8,128)(2,1)S(1)} %shard_map.99.refs_0_.refs_8_), channel_id=1, source_target_pairs={{0,2},{2,4},{4,6},{6,8},{8,10},{10,12},{12,14},{14,0},{1,15},{3,1}... | collective-permute-start | bytes 393224 | tf_op jit(solution)/shard_map/ppermute | solution.py:218
  87.7 5.0 %collective-permute-start.15 = (bf16[2,128,256]{2,1,0:T(8,128)(2,1)S(1)}, bf16[2,128,256]{2,1,0:T(8,128)(2,1)S(1)}, u32[]{:S(2)}, u32[]{:S(2)}) collective-permute-start(bf16[2,128,256]{2,1,0:T(8,128)(2,1)S(1)} %collective-permute-done.14.refs_1_.refs_9_), channel_id=1, source_target_pairs={{0,2},{2,4},{4,6},{6,8},{8,10},{10,12},{12,14},{14,0},{1,15},{3,1}... | collective-permute-start | bytes 393224 | tf_op jit(solution)/shard_map/ppermute | solution.py:218
  92.8 5.0 %collective-permute-start.16 = (bf16[2,128,256]{2,1,0:T(8,128)(2,1)S(1)}, bf16[2,128,256]{2,1,0:T(8,128)(2,1)S(1)}, u32[]{:S(2)}, u32[]{:S(2)}) collective-permute-start(bf16[2,128,256]{2,1,0:T(8,128)(2,1)S(1)} %collective-permute-done.15.refs_2_.refs_10_), channel_id=1, source_target_pairs={{0,2},{2,4},{4,6},{6,8},{8,10},{10,12},{12,14},{14,0},{1,15},{3,1}... | collective-permute-start | bytes 393224 | tf_op jit(solution)/shard_map/ppermute | solution.py:218
  95.8 5.8 %collective-permute-start.18 = (bf16[2,128,256]{2,1,0:T(8,128)(2,1)S(1)}, bf16[2,128,256]{2,1,0:T(8,128)(2,1)S(1)}, u32[]{:S(2)}, u32[]{:S(2)}) collective-permute-start(bf16[2,128,256]{2,1,0:T(8,128)(2,1)S(1)} %collective-permute-done.14.refs_1_.refs_9_), channel_id=1, source_target_pairs={{0,1},{1,0},{2,3},{3,2},{4,5},{5,4},{6,7},{7,6},{8,9},{9,8},{10,11... | collective-permute-start | bytes 393224 | tf_op jit(solution)/shard_map/ppermute | solution.py:220
  95.8 5.8 %collective-permute-start.19 = (bf16[2,128,256]{2,1,0:T(8,128)(2,1)S(1)}, bf16[2,128,256]{2,1,0:T(8,128)(2,1)S(1)}, u32[]{:S(2)}, u32[]{:S(2)}) collective-permute-start(bf16[2,128,256]{2,1,0:T(8,128)(2,1)S(1)} %collective-permute-done.15.refs_2_.refs_10_), channel_id=1, source_target_pairs={{0,1},{1,0},{2,3},{3,2},{4,5},{5,4},{6,7},{7,6},{8,9},{9,8},{10,11... | collective-permute-start | bytes 393224 | tf_op jit(solution)/shard_map/ppermute | solution.py:220
  97.8 5.0 %collective-permute-start.17 = (bf16[2,128,256]{2,1,0:T(8,128)(2,1)S(1)}, bf16[2,128,256]{2,1,0:T(8,128)(2,1)S(1)}, u32[]{:S(2)}, u32[]{:S(2)}) collective-permute-start(bf16[2,128,256]{2,1,0:T(8,128)(2,1)S(1)} %collective-permute-done.16.refs_3_.refs_11_), channel_id=1, source_target_pairs={{0,2},{2,4},{4,6},{6,8},{8,10},{10,12},{12,14},{14,0},{1,15},{3,1}... | collective-permute-start | bytes 393224 | tf_op jit(solution)/shard_map/ppermute | solution.py:218
  109.4 17.1 %all-to-all-start.1 = ((bf16[16,64,256]{2,1,0:T(8,128)(2,1)}), bf16[16,64,256]{2,1,0:T(8,128)(2,1)}, u32[]{:S(2)}, u32[]{:S(2)}) async-start(bf16[16,64,256]{2,1,0:T(8,128)(2,1)} %copy-done.26), calls=%async_computation.1 | async-start | bytes 1048576 | tf_op jit(solution)/shard_map/all_to_all | solution.py:182
  117.4 17.9 %collective-permute-start.11 = (bf16[512,128]{1,0:T(8,128)(2,1)}, bf16[512,128]{1,0:T(8,128)(2,1)}, u32[]{:S(2)}, u32[]{:S(2)}) collective-permute-start(bf16[512,128]{1,0:T(8,128)(2,1)} %copy-done.80), channel_id=1, source_target_pairs={{0,1},{1,2},{2,3},{3,4},{4,5},{5,6},{6,7},{7,8},{8,9},{9,10},{10,1... | collective-permute-start | bytes 393224 | tf_op jit(solution)/shard_map/ppermute | solution.py:223
  122.9 12.4 %collective-permute-start.12 = (bf16[512,128]{1,0:T(8,128)(2,1)}, bf16[512,128]{1,0:T(8,128)(2,1)}, u32[]{:S(2)}, u32[]{:S(2)}) collective-permute-start(bf16[512,128]{1,0:T(8,128)(2,1)} %copy-done.79), channel_id=1, source_target_pairs={{1,0},{2,1},{3,2},{4,3},{5,4},{6,5},{7,6},{8,7},{9,8},{10,9},{11,1... | collective-permute-start | bytes 393224 | tf_op jit(solution)/shard_map/ppermute | solution.py:224
  128.8 16.7 %collective-permute-start.21 = (bf16[64,256]{1,0:T(8,128)(2,1)S(1)}, bf16[64,256]{1,0:T(8,128)(2,1)S(1)}, u32[]{:S(2)}, u32[]{:S(2)}) collective-permute-start(bf16[64,256]{1,0:T(8,128)(2,1)S(1)} %shard_map.102.mine_ref), channel_id=1, source_target_pairs={{0,1},{1,0},{2,3},{3,2},{4,5},{5,4},{6,7},{7,6},{8,9},{9,8},{10,11... | collective-permute-start | bytes 98312 | tf_op jit(solution)/shard_map/ppermute | solution.py:253
  149.7 3.9 %collective-permute-start.25 = (bf16[2,128,256]{2,1,0:T(8,128)(2,1)S(1)}, bf16[2,128,256]{2,1,0:T(8,128)(2,1)S(1)}, u32[]{:S(2)}, u32[]{:S(2)}) collective-permute-start(bf16[2,128,256]{2,1,0:T(8,128)(2,1)S(1)} %shard_map.105.refs_0_.refs_8_), channel_id=1, source_target_pairs={{0,2},{2,4},{4,6},{6,8},{8,10},{10,12},{12,14},{14,0},{1,15},{3,1}... | collective-permute-start | bytes 393224 | tf_op jit(solution)/shard_map/ppermute | solution.py:218
  153.6 5.0 %collective-permute-start.26 = (bf16[2,128,256]{2,1,0:T(8,128)(2,1)S(1)}, bf16[2,128,256]{2,1,0:T(8,128)(2,1)S(1)}, u32[]{:S(2)}, u32[]{:S(2)}) collective-permute-start(bf16[2,128,256]{2,1,0:T(8,128)(2,1)S(1)} %collective-permute-done.25.refs_1_.refs_9_), channel_id=1, source_target_pairs={{0,2},{2,4},{4,6},{6,8},{8,10},{10,12},{12,14},{14,0},{1,15},{3,1}... | collective-permute-start | bytes 393224 | tf_op jit(solution)/shard_map/ppermute | solution.py:218
  158.5 5.0 %collective-permute-start.27 = (bf16[2,128,256]{2,1,0:T(8,128)(2,1)S(1)}, bf16[2,128,256]{2,1,0:T(8,128)(2,1)S(1)}, u32[]{:S(2)}, u32[]{:S(2)}) collective-permute-start(bf16[2,128,256]{2,1,0:T(8,128)(2,1)S(1)} %collective-permute-done.26.refs_2_.refs_10_), channel_id=1, source_target_pairs={{0,2},{2,4},{4,6},{6,8},{8,10},{10,12},{12,14},{14,0},{1,15},{3,1}... | collective-permute-start | bytes 393224 | tf_op jit(solution)/shard_map/ppermute | solution.py:218
  161.6 6.8 %collective-permute-start.29 = (bf16[2,128,256]{2,1,0:T(8,128)(2,1)S(1)}, bf16[2,128,256]{2,1,0:T(8,128)(2,1)S(1)}, u32[]{:S(2)}, u32[]{:S(2)}) collective-permute-start(bf16[2,128,256]{2,1,0:T(8,128)(2,1)S(1)} %collective-permute-done.25.refs_1_.refs_9_), channel_id=1, source_target_pairs={{0,1},{1,0},{2,3},{3,2},{4,5},{5,4},{6,7},{7,6},{8,9},{9,8},{10,11... | collective-permute-start | bytes 393224 | tf_op jit(solution)/shard_map/ppermute | solution.py:220
  162.3 6.2 %collective-permute-start.30 = (bf16[2,128,256]{2,1,0:T(8,128)(2,1)S(1)}, bf16[2,128,256]{2,1,0:T(8,128)(2,1)S(1)}, u32[]{:S(2)}, u32[]{:S(2)}) collective-permute-start(bf16[2,128,256]{2,1,0:T(8,128)(2,1)S(1)} %collective-permute-done.26.refs_2_.refs_10_), channel_id=1, source_target_pairs={{0,1},{1,0},{2,3},{3,2},{4,5},{5,4},{6,7},{7,6},{8,9},{9,8},{10,11... | collective-permute-start | bytes 393224 | tf_op jit(solution)/shard_map/ppermute | solution.py:220
  163.5 5.0 %collective-permute-start.28 = (bf16[2,128,256]{2,1,0:T(8,128)(2,1)S(1)}, bf16[2,128,256]{2,1,0:T(8,128)(2,1)S(1)}, u32[]{:S(2)}, u32[]{:S(2)}) collective-permute-start(bf16[2,128,256]{2,1,0:T(8,128)(2,1)S(1)} %collective-permute-done.27.refs_3_.refs_11_), channel_id=1, source_target_pairs={{0,2},{2,4},{4,6},{6,8},{8,10},{10,12},{12,14},{14,0},{1,15},{3,1}... | collective-permute-start | bytes 393224 | tf_op jit(solution)/shard_map/ppermute | solution.py:218
  175.9 16.3 %all-to-all-start.2 = ((bf16[16,64,256]{2,1,0:T(8,128)(2,1)}), bf16[16,64,256]{2,1,0:T(8,128)(2,1)S(1)}, u32[]{:S(2)}, u32[]{:S(2)}) async-start(bf16[16,64,256]{2,1,0:T(8,128)(2,1)} %copy-done.25), calls=%async_computation.2 | async-start | bytes 1048576 | tf_op jit(solution)/shard_map/all_to_all | solution.py:182
  183.2 17.5 %collective-permute-start.22 = (bf16[512,128]{1,0:T(8,128)(2,1)}, bf16[512,128]{1,0:T(8,128)(2,1)S(1)}, u32[]{:S(2)}, u32[]{:S(2)}) collective-permute-start(bf16[512,128]{1,0:T(8,128)(2,1)} %copy-done.78), channel_id=1, source_target_pairs={{0,1},{1,2},{2,3},{3,4},{4,5},{5,6},{6,7},{7,8},{8,9},{9,10},{10,1... | collective-permute-start | bytes 393224 | tf_op jit(solution)/shard_map/ppermute | solution.py:223
  188.7 12.6 %collective-permute-start.23 = (bf16[512,128]{1,0:T(8,128)(2,1)}, bf16[512,128]{1,0:T(8,128)(2,1)S(1)}, u32[]{:S(2)}, u32[]{:S(2)}) collective-permute-start(bf16[512,128]{1,0:T(8,128)(2,1)} %copy-done.77), channel_id=1, source_target_pairs={{1,0},{2,1},{3,2},{4,3},{5,4},{6,5},{7,6},{8,7},{9,8},{10,9},{11,1... | collective-permute-start | bytes 393224 | tf_op jit(solution)/shard_map/ppermute | solution.py:224
  194.1 18.9 %collective-permute-start.32 = (bf16[64,256]{1,0:T(8,128)(2,1)S(1)}, bf16[64,256]{1,0:T(8,128)(2,1)S(1)}, u32[]{:S(2)}, u32[]{:S(2)}) collective-permute-start(bf16[64,256]{1,0:T(8,128)(2,1)S(1)} %shard_map.108.mine_ref), channel_id=1, source_target_pairs={{0,1},{1,0},{2,3},{3,2},{4,5},{5,4},{6,7},{7,6},{8,9},{9,8},{10,11... | collective-permute-start | bytes 98312 | tf_op jit(solution)/shard_map/ppermute | solution.py:253
  (87 other events, 698.6 us)
where the time goes:
time: 241 us; the launch traced here: 240 us
  starting transfers between devices  113 us (47%)
  local copies, waits for them, and re-layouts  47.4 us (20%)
  waiting for transfers between devices  34.7 us (14%)
  blocking collectives  25.1 us (10%)
  Pallas kernels  19.1 us (8%)
    unnamed x166, local copies, waits for them, and re-layouts  47.4 us
    ppermute x12, starting transfers between devices, shards(): ring.append(lax.ppermute(ring[-1], NARROW, away))  36.5 us
    ppermute x12, waiting for transfers between devices, shards(): ring.append(lax.ppermute(ring[-1], NARROW, away))  29.3 us
    all_to_all x2, blocking collectives, exchanged(): return lax.all_to_all(pieces, axes, split_axis=0, concat_axis=0, tiled=True)  25.1 us
    all_to_all x3, starting transfers between devices, exchanged(): return lax.all_to_all(pieces, axes, split_axis=0, concat_axis=0, tiled=True)  22.2 us
    ppermute x3, starting transfers between devices, shards(): theirs = lax.ppermute(mine, 'narrow_1', swap)  19.7 us
    pallas_call x21, Pallas kernels, call(): pl.pallas_call(kernel, out_shape=[jax.ShapeDtypeStruct(s, d) for s, d in...  19.1 us
    ppermute x3, starting transfers between devices, shards(): low_in = lax.ppermute(high, ALL, up)  16.7 us
  transfers between devices with their start and end apart: 36, of which 18 were waited for; matrix products, arithmetic and copies ran while one was open for 0% of the time, Pallas kernels for 6%

commit v1 on v0

--- a/solution.py
+++ b/solution.py
@@ -36,8 +36,14 @@
     return slice(b * BLK, (b + 1) * BLK)
 
 
+def send(total, transfer_ref, load_ref):
+    coeff = total.astype(BF16)
+    load_ref[0] = coeff
+    load_ref[1] = dot_nn(coeff, transfer_ref[...]).astype(BF16)
+
+
 def begin_kernel(vec_ref, basis_ref, transfer_ref, v_ref, load_ref, low_ref, high_ref):
-    blocks, rank = vec_ref.shape[0] // BLK, basis_ref.shape[1]
+    blocks = vec_ref.shape[0] // BLK
     total = None
     for b in range(blocks):
         t = vec_ref[block(b), :]
@@ -49,8 +55,7 @@
             high_ref[...] = v
         term = dot_nn(t.T.astype(BF16), basis_ref[block(b), :])
         total = term if total is None else total + term
-    load_ref[:rank] = transfer_ref[...]
-    load_ref[rank:] = total.astype(BF16)
+    send(total, transfer_ref, load_ref)
 
 
 def near_kernel(first, blocks_ref, v_ref, low_ref, high_ref, t_ref, shift_ref, *rest):
@@ -66,15 +71,13 @@
         out_ref[block(b), :] = value
 
 
-def share_kernel(base, count, *refs):
-    matrices, loads, out_ref = refs[:count], refs[count:-1], refs[-1]
-    half, rank = out_ref.shape[1:]
-    start = pl.multiple_of(base + lax.axis_index("narrow_1") * half, half)
-    total = None
-    for matrix_ref, load_ref in zip(matrices, loads):
-        for slot in range(2):
-            term = dot_nn(load_ref[slot, pl.ds(start, half), :], matrix_ref[slot, :rank, :])
-            total = term if total is None else total + term
+def share_kernel(*refs):
+    loads, out_ref = refs[:-1], refs[-1]
+    half = out_ref.shape[1]
+    rows = pl.ds(pl.multiple_of(lax.axis_index("narrow_1") * half, half), half)
+    total = loads[0][2, rows, :].astype(F32)
+    for load_ref in loads[1:]:
+        total = total + load_ref[2, rows, :].astype(F32)
     total = total.astype(BF16)
     for copy in range(out_ref.shape[0]):
         out_ref[copy] = total
@@ -88,15 +91,16 @@
 
 
 def pair_kernel(own_ref, other_ref, out_ref):
-    out_ref[0] = own_ref[...]
-    out_ref[1] = other_ref[...]
-
-
-def sibling_kernel(base, count, partner_ref, *refs):
+    out_ref[0] = own_ref[0]
+    out_ref[1] = other_ref[0]
+    out_ref[2] = (own_ref[1].astype(F32) + other_ref[1].astype(F32)).astype(BF16)
+
+
+def sibling_kernel(count, partner_ref, *refs):
     loads, (coupling_ref, out_ref, held) = refs[:count], refs[count:]
     for k, load_ref in enumerate(loads):
         for slot in range(2):
-            held[2 * k + slot] = load_ref[slot, base:, :]
+            held[2 * k + slot] = load_ref[slot]
     chips = lax.axis_size("narrow_0")
     chip, core = lax.axis_index("narrow_0"), lax.axis_index("narrow_1")
     half = chips // 2
@@ -140,7 +144,7 @@
             high_ref[...] = v
         term = dot_nn(t.T.astype(BF16), basis)
         total = term if total is None else total + term
-    load_ref[...] = total.astype(BF16)
+    send(total, transfer_ref, load_ref)
 
 
 def final_kernel(scale, part_ref, far_ref, mine_ref, theirs_ref, transfer_ref, basis_ref, out_ref, squares_ref):
@@ -197,29 +201,28 @@
     swap = [(0, 1), (1, 0)]
     count = chips
 
-    def state(size):
-        return [((rows, cols), BF16), ((size, rank), BF16), ((BLK, cols), BF16), ((BLK, cols), BF16)]
+    state = [((rows, cols), BF16), ((2, cols, rank), BF16), ((BLK, cols), BF16), ((BLK, cols), BF16)]
 
     leaf_flops = 2 * 2 * rows * rank * cols
 
-    away = [(2 * c, 2 * ((c + 1) % chips)) for c in range(chips)]
-    away += [(2 * c + 1, 2 * ((c - 1) % chips) + 1) for c in range(chips)]
+
+    def away(far):
+        there = [(2 * c, 2 * ((c + far) % chips)) for c in range(chips)]
+        return there + [(2 * c + 1, 2 * ((c - far) % chips) + 1) for c in range(chips)]
 
     previous, t = None, vectors
-    v, load, low, high = call(begin_kernel, state(rank + cols), (vectors, leaf_basis, matrix), flops=leaf_flops)
-    matrices = None
+    v, load, low, high = call(begin_kernel, state, (vectors, leaf_basis, matrix), flops=leaf_flops)
     for step in range(DEGREE):
         scale = 1.0 if step == 0 else 2.0
-        base = rank if step == 0 else 0
         partner = lax.ppermute(load, "narrow_1", swap)
-        (pair,) = call(pair_kernel, [((2, *load.shape), BF16)], (load, partner))
+        (pair,) = call(pair_kernel, [((3, cols, rank), BF16)], (load, partner))
         ring, crossed = [pair], []
         for s in range(1, chips // 2 + 1):
-            ring.append(lax.ppermute(ring[-1], NARROW, away))
+            start = 0 if s < 3 else 2
+            ring.append(lax.ppermute(ring[start], NARROW, away(s - start)))
             if s < chips // 2:
                 crossed.append(lax.ppermute(ring[-1], "narrow_1", swap))
         loads = ring + crossed
-        matrices = loads if matrices is None else matrices
         low_in = lax.ppermute(high, ALL, up)
         high_in = lax.ppermute(low, ALL, down)
         operands = [near_blocks, v, low_in, high_in, t, shift] + ([] if previous is None else [previous])
@@ -229,14 +232,9 @@
             operands,
             flops=2 * 3 * blocks * BLK * BLK * cols,
         )
-        (share,) = call(
-            functools.partial(share_kernel, base, count),
-            [((n_wide, half, rank), BF16)],
-            matrices + loads,
-            flops=2 * n_narrow * half * rank * rank,
-        )
+        (share,) = call(share_kernel, [((n_wide, half, rank), BF16)], loads)
         (far,) = call(
-            functools.partial(sibling_kernel, base, count),
+            functools.partial(sibling_kernel, count),
             [((cols, rank), F32)],
             (leaf_partners[0], *loads, leaf_coupling[0]),
             [SMEM] + [VMEM] * (count + 1),
@@ -255,10 +253,7 @@
         previous = t
         if step < DEGREE - 1:
             t, v, load, low, high = call(
-                functools.partial(step_kernel, scale),
-                [((rows, cols), F32)] + state(cols),
-                operands,
-                flops=2 * leaf_flops,
+                functools.partial(step_kernel, scale), [((rows, cols), F32)] + state, operands, flops=2 * leaf_flops
             )
         else:
             out, squares = call(

time: 241 us -> 209 us (0.87)
  starting transfers between devices: 113 us -> 95.2 us
  waiting for transfers between devices: 34.7 us -> 24.7 us
  local copies, waits for them, and re-layouts: 47.4 us -> 40.5 us
    ppermute x12, waiting for transfers between devices: 29.3 us -> 14.4 us  [shards(): ring.append(lax.ppermute(ring[start], NARROW, away(s - start)))]
    ppermute x3, starting transfers between devices: 19.7 us -> 12.1 us  [shards(): theirs = lax.ppermute(mine, 'narrow_1', swap)]
    unnamed x166, local copies, waits for them, and re-layouts: 47.4 us -> 40.5 us
    ppermute x12, starting transfers between devices: 36.5 us -> 30.2 us  [shards(): ring.append(lax.ppermute(ring[start], NARROW, away(s - start)))]
    all_to_all x3, waiting for transfers between devices: 0.97 us -> 6.67 us  [exchanged(): return lax.all_to_all(pieces, axes, split_axis=0, concat_axis=0, tiled=True)]
    ppermute x9, starting transfers between devices: 5.23 us -> 8.68 us  [shards(): crossed.append(lax.ppermute(ring[-1], 'narrow_1', swap))]
    ppermute x3, starting transfers between devices: 9.33 us -> 6.01 us  [shards(): high_in = lax.ppermute(low, ALL, down)]
  transfers between devices with their start and end apart: 36 -> 36, of which waited for: 18 -> 15; matrix products, arithmetic and copies ran while one was open for 0% -> 0% of each run, Pallas kernels for 6% -> 7%
where the time goes in v1:
time: 209 us; the launch traced here: 208 us
  starting transfers between devices  95.2 us (46%)
  local copies, waits for them, and re-layouts  40.5 us (19%)
  blocking collectives  26.1 us (12%)
  waiting for transfers between devices  24.7 us (12%)
  Pallas kernels  20.7 us (10%)
    unnamed x166, local copies, waits for them, and re-layouts  40.5 us
    ppermute x12, starting transfers between devices, shards(): ring.append(lax.ppermute(ring[start], NARROW, away(s - start)))  30.2 us
    all_to_all x2, blocking collectives, exchanged(): return lax.all_to_all(pieces, axes, split_axis=0, concat_axis=0, tiled=True)  26.1 us
    pallas_call x21, Pallas kernels, call(): pl.pallas_call(kernel, out_shape=[jax.ShapeDtypeStruct(s, d) for s, d in...  20.7 us
    all_to_all x3, starting transfers between devices, exchanged(): return lax.all_to_all(pieces, axes, split_axis=0, concat_axis=0, tiled=True)  20.1 us
    ppermute x3, starting transfers between devices, shards(): low_in = lax.ppermute(high, ALL, up)  14.9 us
    ppermute x12, waiting for transfers between devices, shards(): ring.append(lax.ppermute(ring[start], NARROW, away(s - start)))  14.4 us
    ppermute x3, starting transfers between devices, shards(): theirs = lax.ppermute(mine, 'narrow_1', swap)  12.1 us
  transfers between devices with their start and end apart: 36, of which 15 were waited for; matrix products, arithmetic and copies ran while one was open for 0% of the time, Pallas kernels for 7%

profile of v1, /device:TPU:1, one launch (start us, length us, event | category | flops | bytes accessed | tf_op | source)
XLA Modules:
  0.0 207.9 jit_solution(15575407871889715032)
XLA Ops:
  6.0 3.2 %collective-permute-start.2 = (bf16[2,128,256]{2,1,0:T(8,128)(2,1)S(1)}, bf16[2,128,256]{2,1,0:T(8,128)(2,1)S(1)}, u32[]{:S(2)}, u32[]{:S(2)}) collective-permute-start(bf16[2,128,256]{2,1,0:T(8,128)(2,1)S(1)} %get-tuple-element.24.own_ref), channel_id=1, source_target_pairs={{0,1},{1,0},{2,3},{3,2},{4,5},{5,4},{6,7},{7,6},{8,9},{9,8},{10,11... | collective-permute-start | bytes 393224 | tf_op jit(solution)/shard_map/ppermute | solution.py:217
  10.2 4.4 %collective-permute-start.4 = (bf16[3,128,256]{2,1,0:T(8,128)(2,1)S(1)}, bf16[3,128,256]{2,1,0:T(8,128)(2,1)S(1)}, u32[]{:S(2)}, u32[]{:S(2)}) collective-permute-start(bf16[3,128,256]{2,1,0:T(8,128)(2,1)S(1)} %shard_map.93.refs_0_), channel_id=1, source_target_pairs={{0,4},{2,6},{4,8},{6,10},{8,12},{10,14},{12,0},{14,2},{1,13},{3,15... | collective-permute-start | bytes 589832 | tf_op jit(solution)/shard_map/ppermute | solution.py:222
  15.3 2.8 %collective-permute-done.4.refs_2_ = bf16[3,128,256]{2,1,0:T(8,128)(2,1)S(1)} collective-permute-done((bf16[3,128,256]{2,1,0:T(8,128)(2,1)S(1)}, bf16[3,128,256]{2,1,0:T(8,128)(2,1)S(1)}, u32[]{:S(2)}, u32[]{:S(2)}) %collective-permute-start.4) | collective-permute-done | bytes 196640 | tf_op jit(solution)/shard_map/ppermute | solution.py:222
  18.1 4.3 %collective-permute-start.5 = (bf16[3,128,256]{2,1,0:T(8,128)(2,1)S(1)}, bf16[3,128,256]{2,1,0:T(8,128)(2,1)S(1)}, u32[]{:S(2)}, u32[]{:S(2)}) collective-permute-start(bf16[3,128,256]{2,1,0:T(8,128)(2,1)S(1)} %collective-permute-done.4.refs_2_), channel_id=1, source_target_pairs={{0,2},{2,4},{4,6},{6,8},{8,10},{10,12},{12,14},{14,0},{1,15},{3,1}... | collective-permute-start | bytes 589832 | tf_op jit(solution)/shard_map/ppermute | solution.py:222
  30.9 6.7 %all-to-all-start = ((bf16[16,64,256]{2,1,0:T(8,128)(2,1)}), bf16[16,64,256]{2,1,0:T(8,128)(2,1)S(1)}, u32[]{:S(2)}, u32[]{:S(2)}) async-start(bf16[16,64,256]{2,1,0:T(8,128)(2,1)} %shard_map.95), calls=%async_computation | async-start | bytes 1048576 | tf_op jit(solution)/shard_map/all_to_all | solution.py:186
  37.5 6.4 %collective-permute-start = (bf16[512,128]{1,0:T(8,128)(2,1)}, bf16[512,128]{1,0:T(8,128)(2,1)S(1)}, u32[]{:S(2)}, u32[]{:S(2)}) collective-permute-start(bf16[512,128]{1,0:T(8,128)(2,1)} %copy-done.82), channel_id=1, source_target_pairs={{0,1},{1,2},{2,3},{3,4},{4,5},{5,6},{6,7},{7,8},{8,9},{9,10},{10,1... | collective-permute-start | bytes 393224 | tf_op jit(solution)/shard_map/ppermute | solution.py:226
  49.0 4.6 %collective-permute-start.10 = (bf16[64,256]{1,0:T(8,128)(2,1)S(1)}, bf16[64,256]{1,0:T(8,128)(2,1)S(1)}, u32[]{:S(2)}, u32[]{:S(2)}) collective-permute-start(bf16[64,256]{1,0:T(8,128)(2,1)S(1)} %shard_map.96.mine_ref), channel_id=1, source_target_pairs={{0,1},{1,0},{2,3},{3,2},{4,5},{5,4},{6,7},{7,6},{8,9},{9,8},{10,11... | collective-permute-start | bytes 98312 | tf_op jit(solution)/shard_map/ppermute | solution.py:251
  53.7 2.8 %copy-done = bf16[4,3,512,512]{3,2,1,0:T(8,128)(2,1)S(1)} copy-done((bf16[4,3,512,512]{3,2,1,0:T(8,128)(2,1)S(1)}, bf16[4,3,512,512]{3,2,1,0:T(8,128)(2,1)}, u32[]{:S(2)}) %copy-start) | copy-done | bytes 6291480
  57.6 2.8 %shard_map.92.part_ref = f32[2048,128]{1,0:T(8,128)S(1)} custom-call(bf16[4,3,512,512]{3,2,1,0:T(8,128)(2,1)S(1)} %copy-done, bf16[2048,128]{1,0:T(8,128)(2,1)S(1)} %copy-done.72, bf16[512,128]{1,0:T(8,128)(2,1)S(1)} %collective-permute-done.low_ref, bf16[512,128]{1,0:T(8,128)(2,1)} %collective-permute-done.1.high_ref, f32[2048,128]{1,0:T(8,128)S(1)} %copy-done.6, ...), custom_call_target="tpu_custom_call" | custom-call | flops 805306368 | bytes 1000000 | tf_op jit(solution)/shard_map/pallas_call | solution.py:174
  66.5 4.0 %collective-permute-start.15 = (bf16[3,128,256]{2,1,0:T(8,128)(2,1)S(1)}, bf16[3,128,256]{2,1,0:T(8,128)(2,1)S(1)}, u32[]{:S(2)}, u32[]{:S(2)}) collective-permute-start(bf16[3,128,256]{2,1,0:T(8,128)(2,1)S(1)} %shard_map.99.refs_0_), channel_id=1, source_target_pairs={{0,4},{2,6},{4,8},{6,10},{8,12},{10,14},{12,0},{14,2},{1,13},{3,15... | collective-permute-start | bytes 589832 | tf_op jit(solution)/shard_map/ppermute | solution.py:222
  70.6 2.2 %collective-permute-start.14 = (bf16[3,128,256]{2,1,0:T(8,128)(2,1)S(1)}, bf16[3,128,256]{2,1,0:T(8,128)(2,1)S(1)}, u32[]{:S(2)}, u32[]{:S(2)}) collective-permute-start(bf16[3,128,256]{2,1,0:T(8,128)(2,1)S(1)} %shard_map.99.refs_0_), channel_id=1, source_target_pairs={{0,2},{2,4},{4,6},{6,8},{8,10},{10,12},{12,14},{14,0},{1,15},{3,1}... | collective-permute-start | bytes 589832 | tf_op jit(solution)/shard_map/ppermute | solution.py:222
  72.7 2.5 %collective-permute-done.15.refs_2_ = bf16[3,128,256]{2,1,0:T(8,128)(2,1)S(1)} collective-permute-done((bf16[3,128,256]{2,1,0:T(8,128)(2,1)S(1)}, bf16[3,128,256]{2,1,0:T(8,128)(2,1)S(1)}, u32[]{:S(2)}, u32[]{:S(2)}) %collective-permute-start.15) | collective-permute-done | bytes 196640 | tf_op jit(solution)/shard_map/ppermute | solution.py:222
  78.2 2.3 %collective-permute-start.17 = (bf16[3,128,256]{2,1,0:T(8,128)(2,1)S(1)}, bf16[3,128,256]{2,1,0:T(8,128)(2,1)S(1)}, u32[]{:S(2)}, u32[]{:S(2)}) collective-permute-start(bf16[3,128,256]{2,1,0:T(8,128)(2,1)S(1)} %collective-permute-done.15.refs_2_), channel_id=1, source_target_pairs={{0,4},{2,6},{4,8},{6,10},{8,12},{10,14},{12,0},{14,2},{1,13},{3,15... | collective-permute-start | bytes 589832 | tf_op jit(solution)/shard_map/ppermute | solution.py:222
  80.7 2.2 %collective-permute-start.20 = (bf16[3,128,256]{2,1,0:T(8,128)(2,1)S(1)}, bf16[3,128,256]{2,1,0:T(8,128)(2,1)S(1)}, u32[]{:S(2)}, u32[]{:S(2)}) collective-permute-start(bf16[3,128,256]{2,1,0:T(8,128)(2,1)S(1)} %collective-permute-done.16.refs_3_), channel_id=1, source_target_pairs={{0,1},{1,0},{2,3},{3,2},{4,5},{5,4},{6,7},{7,6},{8,9},{9,8},{10,11... | collective-permute-start | bytes 589832 | tf_op jit(solution)/shard_map/ppermute | solution.py:224
  90.8 5.5 %all-to-all-start.1 = ((bf16[16,64,256]{2,1,0:T(8,128)(2,1)}), bf16[16,64,256]{2,1,0:T(8,128)(2,1)}, u32[]{:S(2)}, u32[]{:S(2)}) async-start(bf16[16,64,256]{2,1,0:T(8,128)(2,1)} %copy-done.15), calls=%async_computation.1 | async-start | bytes 1048576 | tf_op jit(solution)/shard_map/all_to_all | solution.py:186
  96.4 4.1 %collective-permute-start.11 = (bf16[512,128]{1,0:T(8,128)(2,1)}, bf16[512,128]{1,0:T(8,128)(2,1)S(1)}, u32[]{:S(2)}, u32[]{:S(2)}) collective-permute-start(bf16[512,128]{1,0:T(8,128)(2,1)} %copy-done.79), channel_id=1, source_target_pairs={{0,1},{1,2},{2,3},{3,4},{4,5},{5,6},{6,7},{7,8},{8,9},{9,10},{10,1... | collective-permute-start | bytes 393224 | tf_op jit(solution)/shard_map/ppermute | solution.py:226
  100.5 2.2 %collective-permute-start.12 = (bf16[512,128]{1,0:T(8,128)(2,1)}, bf16[512,128]{1,0:T(8,128)(2,1)}, u32[]{:S(2)}, u32[]{:S(2)}) collective-permute-start(bf16[512,128]{1,0:T(8,128)(2,1)} %copy-done.77), channel_id=1, source_target_pairs={{1,0},{2,1},{3,2},{4,3},{5,4},{6,5},{7,6},{8,7},{9,8},{10,9},{11,1... | collective-permute-start | bytes 393224 | tf_op jit(solution)/shard_map/ppermute | solution.py:227
  102.7 2.7 %all-to-all-done.1.got_ref = bf16[16,64,256]{2,1,0:T(8,128)(2,1)} async-done(((bf16[16,64,256]{2,1,0:T(8,128)(2,1)}), bf16[16,64,256]{2,1,0:T(8,128)(2,1)}, u32[]{:S(2)}, u32[]{:S(2)}) %all-to-all-start.1) | async-done | bytes 524320 | tf_op jit(solution)/shard_map/all_to_all | solution.py:186
  106.8 4.3 %collective-permute-start.21 = (bf16[64,256]{1,0:T(8,128)(2,1)S(1)}, bf16[64,256]{1,0:T(8,128)(2,1)S(1)}, u32[]{:S(2)}, u32[]{:S(2)}) collective-permute-start(bf16[64,256]{1,0:T(8,128)(2,1)S(1)} %shard_map.102.mine_ref), channel_id=1, source_target_pairs={{0,1},{1,0},{2,3},{3,2},{4,5},{5,4},{6,7},{7,6},{8,9},{9,8},{10,11... | collective-permute-start | bytes 98312 | tf_op jit(solution)/shard_map/ppermute | solution.py:251
  111.2 2.8 %copy-done.1 = bf16[4,3,512,512]{3,2,1,0:T(8,128)(2,1)S(1)} copy-done((bf16[4,3,512,512]{3,2,1,0:T(8,128)(2,1)S(1)}, bf16[4,3,512,512]{3,2,1,0:T(8,128)(2,1)}, u32[]{:S(2)}) %copy-start.1) | copy-done | bytes 6291480
  116.2 2.8 %shard_map.98.part_ref = f32[2048,128]{1,0:T(8,128)S(1)} custom-call(bf16[4,3,512,512]{3,2,1,0:T(8,128)(2,1)S(1)} %copy-done.1, bf16[2048,128]{1,0:T(8,128)(2,1)S(1)} %copy-done.70, bf16[512,128]{1,0:T(8,128)(2,1)S(1)} %collective-permute-done.11.low_ref, bf16[512,128]{1,0:T(8,128)(2,1)} %collective-permute-done.12.high_ref, f32[2048,128]{1,0:T(8,128)S(1)} %copy-done.9, ...), custom_call_target="tpu_custom_call" | custom-call | flops 805306368 | bytes 1000000 | tf_op jit(solution)/shard_map/pallas_call | solution.py:174
  125.1 3.4 %collective-permute-start.26 = (bf16[3,128,256]{2,1,0:T(8,128)(2,1)S(1)}, bf16[3,128,256]{2,1,0:T(8,128)(2,1)S(1)}, u32[]{:S(2)}, u32[]{:S(2)}) collective-permute-start(bf16[3,128,256]{2,1,0:T(8,128)(2,1)S(1)} %shard_map.105.refs_0_), channel_id=1, source_target_pairs={{0,4},{2,6},{4,8},{6,10},{8,12},{10,14},{12,0},{14,2},{1,13},{3,15... | collective-permute-start | bytes 589832 | tf_op jit(solution)/shard_map/ppermute | solution.py:222
  128.5 2.1 collective-permute-start.25
  130.5 2.7 %collective-permute-done.26.refs_2_ = bf16[3,128,256]{2,1,0:T(8,128)(2,1)S(1)} collective-permute-done((bf16[3,128,256]{2,1,0:T(8,128)(2,1)S(1)}, bf16[3,128,256]{2,1,0:T(8,128)(2,1)S(1)}, u32[]{:S(2)}, u32[]{:S(2)}) %collective-permute-start.26) | collective-permute-done | bytes 196640 | tf_op jit(solution)/shard_map/ppermute | solution.py:222
  149.0 7.9 %all-to-all-start.2 = ((bf16[16,64,256]{2,1,0:T(8,128)(2,1)}), bf16[16,64,256]{2,1,0:T(8,128)(2,1)}, u32[]{:S(2)}, u32[]{:S(2)}) async-start(bf16[16,64,256]{2,1,0:T(8,128)(2,1)} %copy-done.16), calls=%async_computation.2 | async-start | bytes 1048576 | tf_op jit(solution)/shard_map/all_to_all | solution.py:186
  156.9 4.3 %collective-permute-start.22 = (bf16[512,128]{1,0:T(8,128)(2,1)}, bf16[512,128]{1,0:T(8,128)(2,1)S(1)}, u32[]{:S(2)}, u32[]{:S(2)}) collective-permute-start(bf16[512,128]{1,0:T(8,128)(2,1)} %copy-done.80), channel_id=1, source_target_pairs={{0,1},{1,2},{2,3},{3,4},{4,5},{5,6},{6,7},{7,8},{8,9},{9,10},{10,1... | collective-permute-start | bytes 393224 | tf_op jit(solution)/shard_map/ppermute | solution.py:226
  163.1 3.3 %all-to-all-done.2.got_ref = bf16[16,64,256]{2,1,0:T(8,128)(2,1)} async-done(((bf16[16,64,256]{2,1,0:T(8,128)(2,1)}), bf16[16,64,256]{2,1,0:T(8,128)(2,1)}, u32[]{:S(2)}, u32[]{:S(2)}) %all-to-all-start.2) | async-done | bytes 524320 | tf_op jit(solution)/shard_map/all_to_all | solution.py:186
  167.9 3.1 %collective-permute-start.32 = (bf16[64,256]{1,0:T(8,128)(2,1)S(1)}, bf16[64,256]{1,0:T(8,128)(2,1)S(1)}, u32[]{:S(2)}, u32[]{:S(2)}) collective-permute-start(bf16[64,256]{1,0:T(8,128)(2,1)S(1)} %shard_map.108.mine_ref), channel_id=1, source_target_pairs={{0,1},{1,0},{2,3},{3,2},{4,5},{5,4},{6,7},{7,6},{8,9},{9,8},{10,11... | collective-permute-start | bytes 98312 | tf_op jit(solution)/shard_map/ppermute | solution.py:251
  171.0 2.8 %copy-done.2 = bf16[4,3,512,512]{3,2,1,0:T(8,128)(2,1)S(1)} copy-done((bf16[4,3,512,512]{3,2,1,0:T(8,128)(2,1)S(1)}, bf16[4,3,512,512]{3,2,1,0:T(8,128)(2,1)}, u32[]{:S(2)}) %copy-start.2) | copy-done | bytes 6291480
  176.1 2.8 %shard_map.104.part_ref = f32[2048,128]{1,0:T(8,128)S(1)} custom-call(bf16[4,3,512,512]{3,2,1,0:T(8,128)(2,1)S(1)} %copy-done.2, bf16[2048,128]{1,0:T(8,128)(2,1)S(1)} %copy-done.68, bf16[512,128]{1,0:T(8,128)(2,1)S(1)} %collective-permute-done.22.low_ref, bf16[512,128]{1,0:T(8,128)(2,1)} %collective-permute-done.23.high_ref, f32[2048,128]{1,0:T(8,128)S(1)} %copy-done.24, ...), custom_call_target="tpu_custom_call" | custom-call | flops 805306368 | bytes 1000000 | tf_op jit(solution)/shard_map/pallas_call | solution.py:174
  180.7 13.0 %all_to_all.25.got_ref = f32[16,8,128]{2,1,0:T(8,128)S(1)} all-to-all(f32[16,8,128]{2,1,0:T(8,128)S(1)} %get-tuple-element.36), channel_id=1, replica_groups=mesh['wide_0'=4,'wide_1'=4,'narrow_0'=8,'narrow_1'=2] {'narrow_0','narro..., dimensions={0} | all-to-all | bytes 131072 | tf_op jit(solution)/shard_map/all_to_all | solution.py:186
  193.7 13.2 %all_to_all.26.got_ref = f32[16,8,128]{2,1,0:T(8,128)S(1)} all-to-all(f32[16,8,128]{2,1,0:T(8,128)S(1)} %shard_map.110), channel_id=1, replica_groups=mesh['wide_0'=4,'wide_1'=4,'narrow_0'=8,'narrow_1'=2] {'wide_0','wide_1'}, dimensions={0} | all-to-all | bytes 131072 | tf_op jit(solution)/shard_map/all_to_all | solution.py:186
  (229 shorter events, 73.0 us)
Async XLA Ops:
  6.0 4.2 %collective-permute-start.2 = (bf16[2,128,256]{2,1,0:T(8,128)(2,1)S(1)}, bf16[2,128,256]{2,1,0:T(8,128)(2,1)S(1)}, u32[]{:S(2)}, u32[]{:S(2)}) collective-permute-start(bf16[2,128,256]{2,1,0:T(8,128)(2,1)S(1)} %get-tuple-element.24.own_ref), channel_id=1, source_target_pairs={{0,1},{1,0},{2,3},{3,2},{4,5},{5,4},{6,7},{7,6},{8,9},{9,8},{10,11... | collective-permute-start | bytes 393224 | tf_op jit(solution)/shard_map/ppermute | solution.py:217
  10.2 7.9 %collective-permute-start.4 = (bf16[3,128,256]{2,1,0:T(8,128)(2,1)S(1)}, bf16[3,128,256]{2,1,0:T(8,128)(2,1)S(1)}, u32[]{:S(2)}, u32[]{:S(2)}) collective-permute-start(bf16[3,128,256]{2,1,0:T(8,128)(2,1)S(1)} %shard_map.93.refs_0_), channel_id=1, source_target_pairs={{0,4},{2,6},{4,8},{6,10},{8,12},{10,14},{12,0},{14,2},{1,13},{3,15... | collective-permute-start | bytes 589832 | tf_op jit(solution)/shard_map/ppermute | solution.py:222
  14.6 9.8 %collective-permute-start.3 = (bf16[3,128,256]{2,1,0:T(8,128)(2,1)S(1)}, bf16[3,128,256]{2,1,0:T(8,128)(2,1)S(1)}, u32[]{:S(2)}, u32[]{:S(2)}) collective-permute-start(bf16[3,128,256]{2,1,0:T(8,128)(2,1)S(1)} %shard_map.93.refs_0_), channel_id=1, source_target_pairs={{0,2},{2,4},{4,6},{6,8},{8,10},{10,12},{12,14},{14,0},{1,15},{3,1}... | collective-permute-start | bytes 589832 | tf_op jit(solution)/shard_map/ppermute | solution.py:222
  18.1 6.9 %collective-permute-start.5 = (bf16[3,128,256]{2,1,0:T(8,128)(2,1)S(1)}, bf16[3,128,256]{2,1,0:T(8,128)(2,1)S(1)}, u32[]{:S(2)}, u32[]{:S(2)}) collective-permute-start(bf16[3,128,256]{2,1,0:T(8,128)(2,1)S(1)} %collective-permute-done.4.refs_2_), channel_id=1, source_target_pairs={{0,2},{2,4},{4,6},{6,8},{8,10},{10,12},{12,14},{14,0},{1,15},{3,1}... | collective-permute-start | bytes 589832 | tf_op jit(solution)/shard_map/ppermute | solution.py:222
  22.4 4.4 %collective-permute-start.8 = (bf16[3,128,256]{2,1,0:T(8,128)(2,1)S(1)}, bf16[3,128,256]{2,1,0:T(8,128)(2,1)S(1)}, u32[]{:S(2)}, u32[]{:S(2)}) collective-permute-start(bf16[3,128,256]{2,1,0:T(8,128)(2,1)S(1)} %collective-permute-done.4.refs_2_), channel_id=1, source_target_pairs={{0,1},{1,0},{2,3},{3,2},{4,5},{5,4},{6,7},{7,6},{8,9},{9,8},{10,11... | collective-permute-start | bytes 589832 | tf_op jit(solution)/shard_map/ppermute | solution.py:224
  22.4 5.5 %collective-permute-start.6 = (bf16[3,128,256]{2,1,0:T(8,128)(2,1)S(1)}, bf16[3,128,256]{2,1,0:T(8,128)(2,1)S(1)}, u32[]{:S(2)}, u32[]{:S(2)}) collective-permute-start(bf16[3,128,256]{2,1,0:T(8,128)(2,1)S(1)} %collective-permute-done.4.refs_2_), channel_id=1, source_target_pairs={{0,4},{2,6},{4,8},{6,10},{8,12},{10,14},{12,0},{14,2},{1,13},{3,15... | collective-permute-start | bytes 589832 | tf_op jit(solution)/shard_map/ppermute | solution.py:222
  24.4 3.6 %collective-permute-start.7 = (bf16[3,128,256]{2,1,0:T(8,128)(2,1)S(1)}, bf16[3,128,256]{2,1,0:T(8,128)(2,1)S(1)}, u32[]{:S(2)}, u32[]{:S(2)}) collective-permute-start(bf16[3,128,256]{2,1,0:T(8,128)(2,1)S(1)} %collective-permute-done.3.refs_1_), channel_id=1, source_target_pairs={{0,1},{1,0},{2,3},{3,2},{4,5},{5,4},{6,7},{7,6},{8,9},{9,8},{10,11... | collective-permute-start | bytes 589832 | tf_op jit(solution)/shard_map/ppermute | solution.py:224
  30.9 15.7 %all-to-all-start = ((bf16[16,64,256]{2,1,0:T(8,128)(2,1)}), bf16[16,64,256]{2,1,0:T(8,128)(2,1)S(1)}, u32[]{:S(2)}, u32[]{:S(2)}) async-start(bf16[16,64,256]{2,1,0:T(8,128)(2,1)} %shard_map.95), calls=%async_computation | async-start | bytes 1048576 | tf_op jit(solution)/shard_map/all_to_all | solution.py:186
  37.5 16.1 %collective-permute-start = (bf16[512,128]{1,0:T(8,128)(2,1)}, bf16[512,128]{1,0:T(8,128)(2,1)S(1)}, u32[]{:S(2)}, u32[]{:S(2)}) collective-permute-start(bf16[512,128]{1,0:T(8,128)(2,1)} %copy-done.82), channel_id=1, source_target_pairs={{0,1},{1,2},{2,3},{3,4},{4,5},{5,6},{6,7},{7,8},{8,9},{9,10},{10,1... | collective-permute-start | bytes 393224 | tf_op jit(solution)/shard_map/ppermute | solution.py:226
  44.0 9.7 %collective-permute-start.1 = (bf16[512,128]{1,0:T(8,128)(2,1)}, bf16[512,128]{1,0:T(8,128)(2,1)}, u32[]{:S(2)}, u32[]{:S(2)}) collective-permute-start(bf16[512,128]{1,0:T(8,128)(2,1)} %copy-done.81), channel_id=1, source_target_pairs={{1,0},{2,1},{3,2},{4,3},{5,4},{6,5},{7,6},{8,7},{9,8},{10,9},{11,1... | collective-permute-start | bytes 393224 | tf_op jit(solution)/shard_map/ppermute | solution.py:227
  49.0 12.5 %collective-permute-start.10 = (bf16[64,256]{1,0:T(8,128)(2,1)S(1)}, bf16[64,256]{1,0:T(8,128)(2,1)S(1)}, u32[]{:S(2)}, u32[]{:S(2)}) collective-permute-start(bf16[64,256]{1,0:T(8,128)(2,1)S(1)} %shard_map.96.mine_ref), channel_id=1, source_target_pairs={{0,1},{1,0},{2,3},{3,2},{4,5},{5,4},{6,7},{7,6},{8,9},{9,8},{10,11... | collective-permute-start | bytes 98312 | tf_op jit(solution)/shard_map/ppermute | solution.py:251
  66.5 8.8 %collective-permute-start.15 = (bf16[3,128,256]{2,1,0:T(8,128)(2,1)S(1)}, bf16[3,128,256]{2,1,0:T(8,128)(2,1)S(1)}, u32[]{:S(2)}, u32[]{:S(2)}) collective-permute-start(bf16[3,128,256]{2,1,0:T(8,128)(2,1)S(1)} %shard_map.99.refs_0_), channel_id=1, source_target_pairs={{0,4},{2,6},{4,8},{6,10},{8,12},{10,14},{12,0},{14,2},{1,13},{3,15... | collective-permute-start | bytes 589832 | tf_op jit(solution)/shard_map/ppermute | solution.py:222
  70.6 10.0 %collective-permute-start.14 = (bf16[3,128,256]{2,1,0:T(8,128)(2,1)S(1)}, bf16[3,128,256]{2,1,0:T(8,128)(2,1)S(1)}, u32[]{:S(2)}, u32[]{:S(2)}) collective-permute-start(bf16[3,128,256]{2,1,0:T(8,128)(2,1)S(1)} %shard_map.99.refs_0_), channel_id=1, source_target_pairs={{0,2},{2,4},{4,6},{6,8},{8,10},{10,12},{12,14},{14,0},{1,15},{3,1}... | collective-permute-start | bytes 589832 | tf_op jit(solution)/shard_map/ppermute | solution.py:222
  75.3 5.5 %collective-permute-start.16 = (bf16[3,128,256]{2,1,0:T(8,128)(2,1)S(1)}, bf16[3,128,256]{2,1,0:T(8,128)(2,1)S(1)}, u32[]{:S(2)}, u32[]{:S(2)}) collective-permute-start(bf16[3,128,256]{2,1,0:T(8,128)(2,1)S(1)} %collective-permute-done.15.refs_2_), channel_id=1, source_target_pairs={{0,2},{2,4},{4,6},{6,8},{8,10},{10,12},{12,14},{14,0},{1,15},{3,1}... | collective-permute-start | bytes 589832 | tf_op jit(solution)/shard_map/ppermute | solution.py:222
  76.6 6.4 %collective-permute-start.19 = (bf16[3,128,256]{2,1,0:T(8,128)(2,1)S(1)}, bf16[3,128,256]{2,1,0:T(8,128)(2,1)S(1)}, u32[]{:S(2)}, u32[]{:S(2)}) collective-permute-start(bf16[3,128,256]{2,1,0:T(8,128)(2,1)S(1)} %collective-permute-done.15.refs_2_), channel_id=1, source_target_pairs={{0,1},{1,0},{2,3},{3,2},{4,5},{5,4},{6,7},{7,6},{8,9},{9,8},{10,11... | collective-permute-start | bytes 589832 | tf_op jit(solution)/shard_map/ppermute | solution.py:224
  78.2 6.3 %collective-permute-start.17 = (bf16[3,128,256]{2,1,0:T(8,128)(2,1)S(1)}, bf16[3,128,256]{2,1,0:T(8,128)(2,1)S(1)}, u32[]{:S(2)}, u32[]{:S(2)}) collective-permute-start(bf16[3,128,256]{2,1,0:T(8,128)(2,1)S(1)} %collective-permute-done.15.refs_2_), channel_id=1, source_target_pairs={{0,4},{2,6},{4,8},{6,10},{8,12},{10,14},{12,0},{14,2},{1,13},{3,15... | collective-permute-start | bytes 589832 | tf_op jit(solution)/shard_map/ppermute | solution.py:222
  80.5 4.0 %collective-permute-start.18 = (bf16[3,128,256]{2,1,0:T(8,128)(2,1)S(1)}, bf16[3,128,256]{2,1,0:T(8,128)(2,1)S(1)}, u32[]{:S(2)}, u32[]{:S(2)}) collective-permute-start(bf16[3,128,256]{2,1,0:T(8,128)(2,1)S(1)} %collective-permute-done.14.refs_1_), channel_id=1, source_target_pairs={{0,1},{1,0},{2,3},{3,2},{4,5},{5,4},{6,7},{7,6},{8,9},{9,8},{10,11... | collective-permute-start | bytes 589832 | tf_op jit(solution)/shard_map/ppermute | solution.py:224
  80.7 3.8 %collective-permute-start.20 = (bf16[3,128,256]{2,1,0:T(8,128)(2,1)S(1)}, bf16[3,128,256]{2,1,0:T(8,128)(2,1)S(1)}, u32[]{:S(2)}, u32[]{:S(2)}) collective-permute-start(bf16[3,128,256]{2,1,0:T(8,128)(2,1)S(1)} %collective-permute-done.16.refs_3_), channel_id=1, source_target_pairs={{0,1},{1,0},{2,3},{3,2},{4,5},{5,4},{6,7},{7,6},{8,9},{9,8},{10,11... | collective-permute-start | bytes 589832 | tf_op jit(solution)/shard_map/ppermute | solution.py:224
  90.8 14.6 %all-to-all-start.1 = ((bf16[16,64,256]{2,1,0:T(8,128)(2,1)}), bf16[16,64,256]{2,1,0:T(8,128)(2,1)}, u32[]{:S(2)}, u32[]{:S(2)}) async-start(bf16[16,64,256]{2,1,0:T(8,128)(2,1)} %copy-done.15), calls=%async_computation.1 | async-start | bytes 1048576 | tf_op jit(solution)/shard_map/all_to_all | solution.py:186
  96.4 14.8 %collective-permute-start.11 = (bf16[512,128]{1,0:T(8,128)(2,1)}, bf16[512,128]{1,0:T(8,128)(2,1)S(1)}, u32[]{:S(2)}, u32[]{:S(2)}) collective-permute-start(bf16[512,128]{1,0:T(8,128)(2,1)} %copy-done.79), channel_id=1, source_target_pairs={{0,1},{1,2},{2,3},{3,4},{4,5},{5,6},{6,7},{7,8},{8,9},{9,10},{10,1... | collective-permute-start | bytes 393224 | tf_op jit(solution)/shard_map/ppermute | solution.py:226
  100.5 10.7 %collective-permute-start.12 = (bf16[512,128]{1,0:T(8,128)(2,1)}, bf16[512,128]{1,0:T(8,128)(2,1)}, u32[]{:S(2)}, u32[]{:S(2)}) collective-permute-start(bf16[512,128]{1,0:T(8,128)(2,1)} %copy-done.77), channel_id=1, source_target_pairs={{1,0},{2,1},{3,2},{4,3},{5,4},{6,5},{7,6},{8,7},{9,8},{10,9},{11,1... | collective-permute-start | bytes 393224 | tf_op jit(solution)/shard_map/ppermute | solution.py:227
  106.8 13.3 %collective-permute-start.21 = (bf16[64,256]{1,0:T(8,128)(2,1)S(1)}, bf16[64,256]{1,0:T(8,128)(2,1)S(1)}, u32[]{:S(2)}, u32[]{:S(2)}) collective-permute-start(bf16[64,256]{1,0:T(8,128)(2,1)S(1)} %shard_map.102.mine_ref), channel_id=1, source_target_pairs={{0,1},{1,0},{2,3},{3,2},{4,5},{5,4},{6,7},{7,6},{8,9},{9,8},{10,11... | collective-permute-start | bytes 98312 | tf_op jit(solution)/shard_map/ppermute | solution.py:251
  125.1 8.1 %collective-permute-start.26 = (bf16[3,128,256]{2,1,0:T(8,128)(2,1)S(1)}, bf16[3,128,256]{2,1,0:T(8,128)(2,1)S(1)}, u32[]{:S(2)}, u32[]{:S(2)}) collective-permute-start(bf16[3,128,256]{2,1,0:T(8,128)(2,1)S(1)} %shard_map.105.refs_0_), channel_id=1, source_target_pairs={{0,4},{2,6},{4,8},{6,10},{8,12},{10,14},{12,0},{14,2},{1,13},{3,15... | collective-permute-start | bytes 589832 | tf_op jit(solution)/shard_map/ppermute | solution.py:222
  128.5 9.9 %collective-permute-start.25 = (bf16[3,128,256]{2,1,0:T(8,128)(2,1)S(1)}, bf16[3,128,256]{2,1,0:T(8,128)(2,1)S(1)}, u32[]{:S(2)}, u32[]{:S(2)}) collective-permute-start(bf16[3,128,256]{2,1,0:T(8,128)(2,1)S(1)} %shard_map.105.refs_0_), channel_id=1, source_target_pairs={{0,2},{2,4},{4,6},{6,8},{8,10},{10,12},{12,14},{14,0},{1,15},{3,1}... | collective-permute-start | bytes 589832 | tf_op jit(solution)/shard_map/ppermute | solution.py:222
  133.2 6.1 %collective-permute-start.27 = (bf16[3,128,256]{2,1,0:T(8,128)(2,1)S(1)}, bf16[3,128,256]{2,1,0:T(8,128)(2,1)S(1)}, u32[]{:S(2)}, u32[]{:S(2)}) collective-permute-start(bf16[3,128,256]{2,1,0:T(8,128)(2,1)S(1)} %collective-permute-done.26.refs_2_), channel_id=1, source_target_pairs={{0,2},{2,4},{4,6},{6,8},{8,10},{10,12},{12,14},{14,0},{1,15},{3,1}... | collective-permute-start | bytes 589832 | tf_op jit(solution)/shard_map/ppermute | solution.py:222
  135.2 5.6 %collective-permute-start.30 = (bf16[3,128,256]{2,1,0:T(8,128)(2,1)S(1)}, bf16[3,128,256]{2,1,0:T(8,128)(2,1)S(1)}, u32[]{:S(2)}, u32[]{:S(2)}) collective-permute-start(bf16[3,128,256]{2,1,0:T(8,128)(2,1)S(1)} %collective-permute-done.26.refs_2_), channel_id=1, source_target_pairs={{0,1},{1,0},{2,3},{3,2},{4,5},{5,4},{6,7},{7,6},{8,9},{9,8},{10,11... | collective-permute-start | bytes 589832 | tf_op jit(solution)/shard_map/ppermute | solution.py:224
  136.8 5.9 %collective-permute-start.28 = (bf16[3,128,256]{2,1,0:T(8,128)(2,1)S(1)}, bf16[3,128,256]{2,1,0:T(8,128)(2,1)S(1)}, u32[]{:S(2)}, u32[]{:S(2)}) collective-permute-start(bf16[3,128,256]{2,1,0:T(8,128)(2,1)S(1)} %collective-permute-done.26.refs_2_), channel_id=1, source_target_pairs={{0,4},{2,6},{4,8},{6,10},{8,12},{10,14},{12,0},{14,2},{1,13},{3,15... | collective-permute-start | bytes 589832 | tf_op jit(solution)/shard_map/ppermute | solution.py:222
  138.3 4.3 %collective-permute-start.29 = (bf16[3,128,256]{2,1,0:T(8,128)(2,1)S(1)}, bf16[3,128,256]{2,1,0:T(8,128)(2,1)S(1)}, u32[]{:S(2)}, u32[]{:S(2)}) collective-permute-start(bf16[3,128,256]{2,1,0:T(8,128)(2,1)S(1)} %collective-permute-done.25.refs_1_), channel_id=1, source_target_pairs={{0,1},{1,0},{2,3},{3,2},{4,5},{5,4},{6,7},{7,6},{8,9},{9,8},{10,11... | collective-permute-start | bytes 589832 | tf_op jit(solution)/shard_map/ppermute | solution.py:224
  149.0 17.4 %all-to-all-start.2 = ((bf16[16,64,256]{2,1,0:T(8,128)(2,1)}), bf16[16,64,256]{2,1,0:T(8,128)(2,1)}, u32[]{:S(2)}, u32[]{:S(2)}) async-start(bf16[16,64,256]{2,1,0:T(8,128)(2,1)} %copy-done.16), calls=%async_computation.2 | async-start | bytes 1048576 | tf_op jit(solution)/shard_map/all_to_all | solution.py:186
  156.9 14.1 %collective-permute-start.22 = (bf16[512,128]{1,0:T(8,128)(2,1)}, bf16[512,128]{1,0:T(8,128)(2,1)S(1)}, u32[]{:S(2)}, u32[]{:S(2)}) collective-permute-start(bf16[512,128]{1,0:T(8,128)(2,1)} %copy-done.80), channel_id=1, source_target_pairs={{0,1},{1,2},{2,3},{3,4},{4,5},{5,6},{6,7},{7,8},{8,9},{9,10},{10,1... | collective-permute-start | bytes 393224 | tf_op jit(solution)/shard_map/ppermute | solution.py:226
  161.2 9.8 %collective-permute-start.23 = (bf16[512,128]{1,0:T(8,128)(2,1)}, bf16[512,128]{1,0:T(8,128)(2,1)}, u32[]{:S(2)}, u32[]{:S(2)}) collective-permute-start(bf16[512,128]{1,0:T(8,128)(2,1)} %copy-done.78), channel_id=1, source_target_pairs={{1,0},{2,1},{3,2},{4,3},{5,4},{6,5},{7,6},{8,7},{9,8},{10,9},{11,1... | collective-permute-start | bytes 393224 | tf_op jit(solution)/shard_map/ppermute | solution.py:227
  167.9 12.1 %collective-permute-start.32 = (bf16[64,256]{1,0:T(8,128)(2,1)S(1)}, bf16[64,256]{1,0:T(8,128)(2,1)S(1)}, u32[]{:S(2)}, u32[]{:S(2)}) collective-permute-start(bf16[64,256]{1,0:T(8,128)(2,1)S(1)} %shard_map.108.mine_ref), channel_id=1, source_target_pairs={{0,1},{1,0},{2,3},{3,2},{4,5},{5,4},{6,7},{7,6},{8,9},{9,8},{10,11... | collective-permute-start | bytes 98312 | tf_op jit(solution)/shard_map/ppermute | solution.py:251
  (87 other events, 748.3 us)

commit v2 on v1

--- a/solution.py
+++ b/solution.py
@@ -42,10 +42,20 @@
     load_ref[1] = dot_nn(coeff, transfer_ref[...]).astype(BF16)
 
 
-def begin_kernel(vec_ref, basis_ref, transfer_ref, v_ref, load_ref, low_ref, high_ref):
+def begin_kernel(
+    vec_hbm, basis_hbm, transfer_hbm, v_ref, load_ref, low_ref, high_ref, vec_ref, basis_ref, transfer_ref, sems
+):
     blocks = vec_ref.shape[0] // BLK
+    copies = []
+    for b in range(blocks):
+        copies.append(pltpu.make_async_copy(vec_hbm.at[block(b), :], vec_ref.at[block(b), :], sems.at[2 * b]))
+        copies.append(pltpu.make_async_copy(basis_hbm.at[block(b), :], basis_ref.at[block(b), :], sems.at[2 * b + 1]))
+    copies.append(pltpu.make_async_copy(transfer_hbm, transfer_ref, sems.at[2 * blocks]))
+    for copy in copies:
+        copy.start()
     total = None
     for b in range(blocks):
+        copies[2 * b].wait()
         t = vec_ref[block(b), :]
         v = t.astype(BF16)
         v_ref[block(b), :] = v
@@ -53,8 +63,10 @@
             low_ref[...] = v
         if b == blocks - 1:
             high_ref[...] = v
+        copies[2 * b + 1].wait()
         term = dot_nn(t.T.astype(BF16), basis_ref[block(b), :])
         total = term if total is None else total + term
+    copies[-1].wait()
     send(total, transfer_ref, load_ref)
 
 
@@ -170,14 +182,14 @@
     out_ref[...] = t_ref[...] / jnp.sqrt(squares / total_rows + 1e-06)
 
 
-def call(kernel, outs, operands, specs=None, flops=1e6, moved=1e6, scratch=()):
+def call(kernel, outs, operands, specs=None, flops=1e6, moved=1e6, scratch=(), mib=16):
     return pl.pallas_call(
         kernel,
         out_shape=[jax.ShapeDtypeStruct(s, d) for s, d in outs],
         in_specs=specs or [VMEM] * len(operands),
         out_specs=[VMEM] * len(outs),
         scratch_shapes=scratch,
-        compiler_params=pltpu.CompilerParams(vmem_limit_bytes=16 * 1024 * 1024),
+        compiler_params=pltpu.CompilerParams(vmem_limit_bytes=mib * 1024 * 1024),
         cost_estimate=cost(flops, moved),
     )(*operands)
 
@@ -200,18 +212,28 @@
     down = [(b, a) for a, b in up]
     swap = [(0, 1), (1, 0)]
     count = chips
-
     state = [((rows, cols), BF16), ((2, cols, rank), BF16), ((BLK, cols), BF16), ((BLK, cols), BF16)]
-
     leaf_flops = 2 * 2 * rows * rank * cols
-
 
     def away(far):
         there = [(2 * c, 2 * ((c + far) % chips)) for c in range(chips)]
         return there + [(2 * c + 1, 2 * ((c - far) % chips) + 1) for c in range(chips)]
 
     previous, t = None, vectors
-    v, load, low, high = call(begin_kernel, state, (vectors, leaf_basis, matrix), flops=leaf_flops)
+    v, load, low, high = call(
+        begin_kernel,
+        state,
+        (vectors, leaf_basis, matrix),
+        [pl.BlockSpec(memory_space=pltpu.HBM)] * 3,
+        flops=leaf_flops,
+        mib=60,
+        scratch=[
+            pltpu.VMEM(vectors.shape, F32),
+            pltpu.VMEM(leaf_basis.shape, BF16),
+            pltpu.VMEM(matrix.shape, BF16),
+            pltpu.SemaphoreType.DMA((2 * blocks + 1,)),
+        ],
+    )
     for step in range(DEGREE):
         scale = 1.0 if step == 0 else 2.0
         partner = lax.ppermute(load, "narrow_1", swap)

time: 209 us -> 207 us (level)
  local copies, waits for them, and re-layouts: 40.5 us -> 37 us
    unnamed x166 -> x160, local copies, waits for them, and re-layouts: 40.5 us -> 37 us
where the time goes in v2:
time: 207 us; the launch traced here: 206 us
  starting transfers between devices  95.1 us (46%)
  local copies, waits for them, and re-layouts  37 us (18%)
  blocking collectives  26.1 us (13%)
  waiting for transfers between devices  25 us (12%)
  Pallas kernels  22 us (11%)
    unnamed x160, local copies, waits for them, and re-layouts  37 us
    ppermute x12, starting transfers between devices, shards(): ring.append(lax.ppermute(ring[start], NARROW, away(s - start)))  30.1 us
    all_to_all x2, blocking collectives, exchanged(): return lax.all_to_all(pieces, axes, split_axis=0, concat_axis=0, tiled=True)  26.1 us
    pallas_call x21, Pallas kernels, call(): pl.pallas_call(kernel, out_shape=[jax.ShapeDtypeStruct(s, d) for s, d in...  22 us
    all_to_all x3, starting transfers between devices, exchanged(): return lax.all_to_all(pieces, axes, split_axis=0, concat_axis=0, tiled=True)  20 us
    ppermute x3, starting transfers between devices, shards(): low_in = lax.ppermute(high, ALL, up)  14.9 us
    ppermute x12, waiting for transfers between devices, shards(): ring.append(lax.ppermute(ring[start], NARROW, away(s - start)))  14.4 us
    ppermute x3, starting transfers between devices, shards(): theirs = lax.ppermute(mine, 'narrow_1', swap)  12.1 us
  transfers between devices with their start and end apart: 36, of which 15 were waited for; matrix products, arithmetic and copies ran while one was open for 0% of the time, Pallas kernels for 7%

profile of v2, /device:TPU:1, one launch (start us, length us, event | category | flops | bytes accessed | tf_op | source)
XLA Modules:
  0.0 205.8 jit_solution(2406494531899488113)
XLA Ops:
  0.0 3.0 %shard_map.91 = (bf16[2048,128]{1,0:T(8,128)(2,1)}, bf16[2,128,256]{2,1,0:T(8,128)(2,1)}, bf16[512,128]{1,0:T(8,128)(2,1)}, bf16[512,128]{1,0:T(8,128)(2,1)}) custom-call(f32[2048,128]{1,0:T(8,128)} %rest_0_.1, bf16[2048,256]{1,0:T(8,128)(2,1)} %basis_ref.5, bf16[256,256]{1,0:T(8,128)(2,1)} %bitcast.12), custom_call_target="tpu_custom_call" | custom-call | flops 268435456 | bytes 1000000 | tf_op jit(solution)/shard_map/pallas_call | solution.py:186
  3.0 3.3 %collective-permute-start.2 = (bf16[2,128,256]{2,1,0:T(8,128)(2,1)}, bf16[2,128,256]{2,1,0:T(8,128)(2,1)S(1)}, u32[]{:S(2)}, u32[]{:S(2)}) collective-permute-start(bf16[2,128,256]{2,1,0:T(8,128)(2,1)} %get-tuple-element.24.own_ref), channel_id=1, source_target_pairs={{0,1},{1,0},{2,3},{3,2},{4,5},{5,4},{6,7},{7,6},{8,9},{9,8},{10,11... | collective-permute-start | bytes 393224 | tf_op jit(solution)/shard_map/ppermute | solution.py:239
  8.5 4.4 %collective-permute-start.4 = (bf16[3,128,256]{2,1,0:T(8,128)(2,1)S(1)}, bf16[3,128,256]{2,1,0:T(8,128)(2,1)S(1)}, u32[]{:S(2)}, u32[]{:S(2)}) collective-permute-start(bf16[3,128,256]{2,1,0:T(8,128)(2,1)S(1)} %shard_map.93.refs_0_), channel_id=1, source_target_pairs={{0,4},{2,6},{4,8},{6,10},{8,12},{10,14},{12,0},{14,2},{1,13},{3,15... | collective-permute-start | bytes 589832 | tf_op jit(solution)/shard_map/ppermute | solution.py:244
  13.6 2.8 %collective-permute-done.4.refs_2_ = bf16[3,128,256]{2,1,0:T(8,128)(2,1)S(1)} collective-permute-done((bf16[3,128,256]{2,1,0:T(8,128)(2,1)S(1)}, bf16[3,128,256]{2,1,0:T(8,128)(2,1)S(1)}, u32[]{:S(2)}, u32[]{:S(2)}) %collective-permute-start.4) | collective-permute-done | bytes 196640 | tf_op jit(solution)/shard_map/ppermute | solution.py:244
  16.4 4.3 %collective-permute-start.5 = (bf16[3,128,256]{2,1,0:T(8,128)(2,1)S(1)}, bf16[3,128,256]{2,1,0:T(8,128)(2,1)S(1)}, u32[]{:S(2)}, u32[]{:S(2)}) collective-permute-start(bf16[3,128,256]{2,1,0:T(8,128)(2,1)S(1)} %collective-permute-done.4.refs_2_), channel_id=1, source_target_pairs={{0,2},{2,4},{4,6},{6,8},{8,10},{10,12},{12,14},{14,0},{1,15},{3,1}... | collective-permute-start | bytes 589832 | tf_op jit(solution)/shard_map/ppermute | solution.py:244
  20.7 1.9 collective-permute-start.6
  29.8 6.7 %all-to-all-start = ((bf16[16,64,256]{2,1,0:T(8,128)(2,1)}), bf16[16,64,256]{2,1,0:T(8,128)(2,1)S(1)}, u32[]{:S(2)}, u32[]{:S(2)}) async-start(bf16[16,64,256]{2,1,0:T(8,128)(2,1)} %shard_map.95), calls=%async_computation | async-start | bytes 1048576 | tf_op jit(solution)/shard_map/all_to_all | solution.py:198
  36.5 6.4 %collective-permute-start = (bf16[512,128]{1,0:T(8,128)(2,1)}, bf16[512,128]{1,0:T(8,128)(2,1)S(1)}, u32[]{:S(2)}, u32[]{:S(2)}) collective-permute-start(bf16[512,128]{1,0:T(8,128)(2,1)} %get-tuple-element.22), channel_id=1, source_target_pairs={{0,1},{1,2},{2,3},{3,4},{4,5},{5,6},{6,7},{7,8},{8,9},{9,10},{10,1... | collective-permute-start | bytes 393224 | tf_op jit(solution)/shard_map/ppermute | solution.py:248
  48.0 4.6 %collective-permute-start.10 = (bf16[64,256]{1,0:T(8,128)(2,1)S(1)}, bf16[64,256]{1,0:T(8,128)(2,1)S(1)}, u32[]{:S(2)}, u32[]{:S(2)}) collective-permute-start(bf16[64,256]{1,0:T(8,128)(2,1)S(1)} %shard_map.96.mine_ref), channel_id=1, source_target_pairs={{0,1},{1,0},{2,3},{3,2},{4,5},{5,4},{6,7},{7,6},{8,9},{9,8},{10,11... | collective-permute-start | bytes 98312 | tf_op jit(solution)/shard_map/ppermute | solution.py:273
  53.3 2.8 %copy-done = bf16[4,3,512,512]{3,2,1,0:T(8,128)(2,1)S(1)} copy-done((bf16[4,3,512,512]{3,2,1,0:T(8,128)(2,1)S(1)}, bf16[4,3,512,512]{3,2,1,0:T(8,128)(2,1)}, u32[]{:S(2)}) %copy-start) | copy-done | bytes 6291480
  65.2 4.0 %collective-permute-start.15 = (bf16[3,128,256]{2,1,0:T(8,128)(2,1)S(1)}, bf16[3,128,256]{2,1,0:T(8,128)(2,1)S(1)}, u32[]{:S(2)}, u32[]{:S(2)}) collective-permute-start(bf16[3,128,256]{2,1,0:T(8,128)(2,1)S(1)} %shard_map.99.refs_0_), channel_id=1, source_target_pairs={{0,4},{2,6},{4,8},{6,10},{8,12},{10,14},{12,0},{14,2},{1,13},{3,15... | collective-permute-start | bytes 589832 | tf_op jit(solution)/shard_map/ppermute | solution.py:244
  69.3 2.2 %collective-permute-start.14 = (bf16[3,128,256]{2,1,0:T(8,128)(2,1)S(1)}, bf16[3,128,256]{2,1,0:T(8,128)(2,1)S(1)}, u32[]{:S(2)}, u32[]{:S(2)}) collective-permute-start(bf16[3,128,256]{2,1,0:T(8,128)(2,1)S(1)} %shard_map.99.refs_0_), channel_id=1, source_target_pairs={{0,2},{2,4},{4,6},{6,8},{8,10},{10,12},{12,14},{14,0},{1,15},{3,1}... | collective-permute-start | bytes 589832 | tf_op jit(solution)/shard_map/ppermute | solution.py:244
  71.5 2.5 %collective-permute-done.15.refs_2_ = bf16[3,128,256]{2,1,0:T(8,128)(2,1)S(1)} collective-permute-done((bf16[3,128,256]{2,1,0:T(8,128)(2,1)S(1)}, bf16[3,128,256]{2,1,0:T(8,128)(2,1)S(1)}, u32[]{:S(2)}, u32[]{:S(2)}) %collective-permute-start.15) | collective-permute-done | bytes 196640 | tf_op jit(solution)/shard_map/ppermute | solution.py:244
  76.9 2.3 %collective-permute-start.17 = (bf16[3,128,256]{2,1,0:T(8,128)(2,1)S(1)}, bf16[3,128,256]{2,1,0:T(8,128)(2,1)S(1)}, u32[]{:S(2)}, u32[]{:S(2)}) collective-permute-start(bf16[3,128,256]{2,1,0:T(8,128)(2,1)S(1)} %collective-permute-done.15.refs_2_), channel_id=1, source_target_pairs={{0,4},{2,6},{4,8},{6,10},{8,12},{10,14},{12,0},{14,2},{1,13},{3,15... | collective-permute-start | bytes 589832 | tf_op jit(solution)/shard_map/ppermute | solution.py:244
  79.5 2.3 %collective-permute-start.20 = (bf16[3,128,256]{2,1,0:T(8,128)(2,1)S(1)}, bf16[3,128,256]{2,1,0:T(8,128)(2,1)S(1)}, u32[]{:S(2)}, u32[]{:S(2)}) collective-permute-start(bf16[3,128,256]{2,1,0:T(8,128)(2,1)S(1)} %collective-permute-done.16.refs_3_), channel_id=1, source_target_pairs={{0,1},{1,0},{2,3},{3,2},{4,5},{5,4},{6,7},{7,6},{8,9},{9,8},{10,11... | collective-permute-start | bytes 589832 | tf_op jit(solution)/shard_map/ppermute | solution.py:246
  89.6 5.4 %all-to-all-start.1 = ((bf16[16,64,256]{2,1,0:T(8,128)(2,1)}), bf16[16,64,256]{2,1,0:T(8,128)(2,1)}, u32[]{:S(2)}, u32[]{:S(2)}) async-start(bf16[16,64,256]{2,1,0:T(8,128)(2,1)} %copy-done.12), calls=%async_computation.1 | async-start | bytes 1048576 | tf_op jit(solution)/shard_map/all_to_all | solution.py:198
  95.0 4.2 %collective-permute-start.11 = (bf16[512,128]{1,0:T(8,128)(2,1)}, bf16[512,128]{1,0:T(8,128)(2,1)S(1)}, u32[]{:S(2)}, u32[]{:S(2)}) collective-permute-start(bf16[512,128]{1,0:T(8,128)(2,1)} %copy-done.78), channel_id=1, source_target_pairs={{0,1},{1,2},{2,3},{3,4},{4,5},{5,6},{6,7},{7,8},{8,9},{9,10},{10,1... | collective-permute-start | bytes 393224 | tf_op jit(solution)/shard_map/ppermute | solution.py:248
  99.3 2.1 %collective-permute-start.12 = (bf16[512,128]{1,0:T(8,128)(2,1)}, bf16[512,128]{1,0:T(8,128)(2,1)}, u32[]{:S(2)}, u32[]{:S(2)}) collective-permute-start(bf16[512,128]{1,0:T(8,128)(2,1)} %copy-done.76), channel_id=1, source_target_pairs={{1,0},{2,1},{3,2},{4,3},{5,4},{6,5},{7,6},{8,7},{9,8},{10,9},{11,1... | collective-permute-start | bytes 393224 | tf_op jit(solution)/shard_map/ppermute | solution.py:249
  101.3 2.7 %all-to-all-done.1.got_ref = bf16[16,64,256]{2,1,0:T(8,128)(2,1)} async-done(((bf16[16,64,256]{2,1,0:T(8,128)(2,1)}), bf16[16,64,256]{2,1,0:T(8,128)(2,1)}, u32[]{:S(2)}, u32[]{:S(2)}) %all-to-all-start.1) | async-done | bytes 524320 | tf_op jit(solution)/shard_map/all_to_all | solution.py:198
  105.5 4.3 %collective-permute-start.21 = (bf16[64,256]{1,0:T(8,128)(2,1)S(1)}, bf16[64,256]{1,0:T(8,128)(2,1)S(1)}, u32[]{:S(2)}, u32[]{:S(2)}) collective-permute-start(bf16[64,256]{1,0:T(8,128)(2,1)S(1)} %shard_map.102.mine_ref), channel_id=1, source_target_pairs={{0,1},{1,0},{2,3},{3,2},{4,5},{5,4},{6,7},{7,6},{8,9},{9,8},{10,11... | collective-permute-start | bytes 98312 | tf_op jit(solution)/shard_map/ppermute | solution.py:273
  109.8 2.8 %copy-done.1 = bf16[4,3,512,512]{3,2,1,0:T(8,128)(2,1)S(1)} copy-done((bf16[4,3,512,512]{3,2,1,0:T(8,128)(2,1)S(1)}, bf16[4,3,512,512]{3,2,1,0:T(8,128)(2,1)}, u32[]{:S(2)}) %copy-start.1) | copy-done | bytes 6291480
  114.9 2.8 %shard_map.98.part_ref = f32[2048,128]{1,0:T(8,128)S(1)} custom-call(bf16[4,3,512,512]{3,2,1,0:T(8,128)(2,1)S(1)} %copy-done.1, bf16[2048,128]{1,0:T(8,128)(2,1)S(1)} %copy-done.67, bf16[512,128]{1,0:T(8,128)(2,1)S(1)} %collective-permute-done.11.low_ref, bf16[512,128]{1,0:T(8,128)(2,1)} %collective-permute-done.12.high_ref, f32[2048,128]{1,0:T(8,128)S(1)} %copy-done.7, ...), custom_call_target="tpu_custom_call" | custom-call | flops 805306368 | bytes 1000000 | tf_op jit(solution)/shard_map/pallas_call | solution.py:186
  123.1 3.7 %collective-permute-start.26 = (bf16[3,128,256]{2,1,0:T(8,128)(2,1)S(1)}, bf16[3,128,256]{2,1,0:T(8,128)(2,1)S(1)}, u32[]{:S(2)}, u32[]{:S(2)}) collective-permute-start(bf16[3,128,256]{2,1,0:T(8,128)(2,1)S(1)} %shard_map.105.refs_0_), channel_id=1, source_target_pairs={{0,4},{2,6},{4,8},{6,10},{8,12},{10,14},{12,0},{14,2},{1,13},{3,15... | collective-permute-start | bytes 589832 | tf_op jit(solution)/shard_map/ppermute | solution.py:244
  128.6 2.8 %collective-permute-done.26.refs_2_ = bf16[3,128,256]{2,1,0:T(8,128)(2,1)S(1)} collective-permute-done((bf16[3,128,256]{2,1,0:T(8,128)(2,1)S(1)}, bf16[3,128,256]{2,1,0:T(8,128)(2,1)S(1)}, u32[]{:S(2)}, u32[]{:S(2)}) %collective-permute-start.26) | collective-permute-done | bytes 196640 | tf_op jit(solution)/shard_map/ppermute | solution.py:244
  147.0 7.8 %all-to-all-start.2 = ((bf16[16,64,256]{2,1,0:T(8,128)(2,1)}), bf16[16,64,256]{2,1,0:T(8,128)(2,1)}, u32[]{:S(2)}, u32[]{:S(2)}) async-start(bf16[16,64,256]{2,1,0:T(8,128)(2,1)} %copy-done.13), calls=%async_computation.2 | async-start | bytes 1048576 | tf_op jit(solution)/shard_map/all_to_all | solution.py:198
  154.9 4.3 %collective-permute-start.22 = (bf16[512,128]{1,0:T(8,128)(2,1)}, bf16[512,128]{1,0:T(8,128)(2,1)S(1)}, u32[]{:S(2)}, u32[]{:S(2)}) collective-permute-start(bf16[512,128]{1,0:T(8,128)(2,1)} %copy-done.79), channel_id=1, source_target_pairs={{0,1},{1,2},{2,3},{3,4},{4,5},{5,6},{6,7},{7,8},{8,9},{9,10},{10,1... | collective-permute-start | bytes 393224 | tf_op jit(solution)/shard_map/ppermute | solution.py:248
  161.1 3.3 %all-to-all-done.2.got_ref = bf16[16,64,256]{2,1,0:T(8,128)(2,1)} async-done(((bf16[16,64,256]{2,1,0:T(8,128)(2,1)}), bf16[16,64,256]{2,1,0:T(8,128)(2,1)}, u32[]{:S(2)}, u32[]{:S(2)}) %all-to-all-start.2) | async-done | bytes 524320 | tf_op jit(solution)/shard_map/all_to_all | solution.py:198
  165.8 3.1 %collective-permute-start.32 = (bf16[64,256]{1,0:T(8,128)(2,1)S(1)}, bf16[64,256]{1,0:T(8,128)(2,1)S(1)}, u32[]{:S(2)}, u32[]{:S(2)}) collective-permute-start(bf16[64,256]{1,0:T(8,128)(2,1)S(1)} %shard_map.108.mine_ref), channel_id=1, source_target_pairs={{0,1},{1,0},{2,3},{3,2},{4,5},{5,4},{6,7},{7,6},{8,9},{9,8},{10,11... | collective-permute-start | bytes 98312 | tf_op jit(solution)/shard_map/ppermute | solution.py:273
  169.0 2.8 %copy-done.2 = bf16[4,3,512,512]{3,2,1,0:T(8,128)(2,1)S(1)} copy-done((bf16[4,3,512,512]{3,2,1,0:T(8,128)(2,1)S(1)}, bf16[4,3,512,512]{3,2,1,0:T(8,128)(2,1)}, u32[]{:S(2)}) %copy-start.2) | copy-done | bytes 6291480
  174.0 2.8 %shard_map.104.part_ref = f32[2048,128]{1,0:T(8,128)S(1)} custom-call(bf16[4,3,512,512]{3,2,1,0:T(8,128)(2,1)S(1)} %copy-done.2, bf16[2048,128]{1,0:T(8,128)(2,1)S(1)} %copy-done.65, bf16[512,128]{1,0:T(8,128)(2,1)S(1)} %collective-permute-done.22.low_ref, bf16[512,128]{1,0:T(8,128)(2,1)} %collective-permute-done.23.high_ref, f32[2048,128]{1,0:T(8,128)S(1)} %copy-done.21, ...), custom_call_target="tpu_custom_call" | custom-call | flops 805306368 | bytes 1000000 | tf_op jit(solution)/shard_map/pallas_call | solution.py:186
  178.6 13.1 %all_to_all.25.got_ref = f32[16,8,128]{2,1,0:T(8,128)S(1)} all-to-all(f32[16,8,128]{2,1,0:T(8,128)S(1)} %get-tuple-element.36), channel_id=1, replica_groups=mesh['wide_0'=4,'wide_1'=4,'narrow_0'=8,'narrow_1'=2] {'narrow_0','narro..., dimensions={0} | all-to-all | bytes 131072 | tf_op jit(solution)/shard_map/all_to_all | solution.py:198
  191.7 13.1 %all_to_all.26.got_ref = f32[16,8,128]{2,1,0:T(8,128)S(1)} all-to-all(f32[16,8,128]{2,1,0:T(8,128)S(1)} %shard_map.110), channel_id=1, replica_groups=mesh['wide_0'=4,'wide_1'=4,'narrow_0'=8,'narrow_1'=2] {'wide_0','wide_1'}, dimensions={0} | all-to-all | bytes 131072 | tf_op jit(solution)/shard_map/all_to_all | solution.py:198
  (223 shorter events, 70.5 us)
Async XLA Ops:
  3.0 4.5 %collective-permute-start.2 = (bf16[2,128,256]{2,1,0:T(8,128)(2,1)}, bf16[2,128,256]{2,1,0:T(8,128)(2,1)S(1)}, u32[]{:S(2)}, u32[]{:S(2)}) collective-permute-start(bf16[2,128,256]{2,1,0:T(8,128)(2,1)} %get-tuple-element.24.own_ref), channel_id=1, source_target_pairs={{0,1},{1,0},{2,3},{3,2},{4,5},{5,4},{6,7},{7,6},{8,9},{9,8},{10,11... | collective-permute-start | bytes 393224 | tf_op jit(solution)/shard_map/ppermute | solution.py:239
  8.5 7.9 %collective-permute-start.4 = (bf16[3,128,256]{2,1,0:T(8,128)(2,1)S(1)}, bf16[3,128,256]{2,1,0:T(8,128)(2,1)S(1)}, u32[]{:S(2)}, u32[]{:S(2)}) collective-permute-start(bf16[3,128,256]{2,1,0:T(8,128)(2,1)S(1)} %shard_map.93.refs_0_), channel_id=1, source_target_pairs={{0,4},{2,6},{4,8},{6,10},{8,12},{10,14},{12,0},{14,2},{1,13},{3,15... | collective-permute-start | bytes 589832 | tf_op jit(solution)/shard_map/ppermute | solution.py:244
  12.9 9.8 %collective-permute-start.3 = (bf16[3,128,256]{2,1,0:T(8,128)(2,1)S(1)}, bf16[3,128,256]{2,1,0:T(8,128)(2,1)S(1)}, u32[]{:S(2)}, u32[]{:S(2)}) collective-permute-start(bf16[3,128,256]{2,1,0:T(8,128)(2,1)S(1)} %shard_map.93.refs_0_), channel_id=1, source_target_pairs={{0,2},{2,4},{4,6},{6,8},{8,10},{10,12},{12,14},{14,0},{1,15},{3,1}... | collective-permute-start | bytes 589832 | tf_op jit(solution)/shard_map/ppermute | solution.py:244
  16.4 6.9 %collective-permute-start.5 = (bf16[3,128,256]{2,1,0:T(8,128)(2,1)S(1)}, bf16[3,128,256]{2,1,0:T(8,128)(2,1)S(1)}, u32[]{:S(2)}, u32[]{:S(2)}) collective-permute-start(bf16[3,128,256]{2,1,0:T(8,128)(2,1)S(1)} %collective-permute-done.4.refs_2_), channel_id=1, source_target_pairs={{0,2},{2,4},{4,6},{6,8},{8,10},{10,12},{12,14},{14,0},{1,15},{3,1}... | collective-permute-start | bytes 589832 | tf_op jit(solution)/shard_map/ppermute | solution.py:244
  20.7 4.4 %collective-permute-start.8 = (bf16[3,128,256]{2,1,0:T(8,128)(2,1)S(1)}, bf16[3,128,256]{2,1,0:T(8,128)(2,1)S(1)}, u32[]{:S(2)}, u32[]{:S(2)}) collective-permute-start(bf16[3,128,256]{2,1,0:T(8,128)(2,1)S(1)} %collective-permute-done.4.refs_2_), channel_id=1, source_target_pairs={{0,1},{1,0},{2,3},{3,2},{4,5},{5,4},{6,7},{7,6},{8,9},{9,8},{10,11... | collective-permute-start | bytes 589832 | tf_op jit(solution)/shard_map/ppermute | solution.py:246
  20.7 5.5 %collective-permute-start.6 = (bf16[3,128,256]{2,1,0:T(8,128)(2,1)S(1)}, bf16[3,128,256]{2,1,0:T(8,128)(2,1)S(1)}, u32[]{:S(2)}, u32[]{:S(2)}) collective-permute-start(bf16[3,128,256]{2,1,0:T(8,128)(2,1)S(1)} %collective-permute-done.4.refs_2_), channel_id=1, source_target_pairs={{0,4},{2,6},{4,8},{6,10},{8,12},{10,14},{12,0},{14,2},{1,13},{3,15... | collective-permute-start | bytes 589832 | tf_op jit(solution)/shard_map/ppermute | solution.py:244
  22.6 3.6 %collective-permute-start.7 = (bf16[3,128,256]{2,1,0:T(8,128)(2,1)S(1)}, bf16[3,128,256]{2,1,0:T(8,128)(2,1)S(1)}, u32[]{:S(2)}, u32[]{:S(2)}) collective-permute-start(bf16[3,128,256]{2,1,0:T(8,128)(2,1)S(1)} %collective-permute-done.3.refs_1_), channel_id=1, source_target_pairs={{0,1},{1,0},{2,3},{3,2},{4,5},{5,4},{6,7},{7,6},{8,9},{9,8},{10,11... | collective-permute-start | bytes 589832 | tf_op jit(solution)/shard_map/ppermute | solution.py:246
  29.8 15.7 %all-to-all-start = ((bf16[16,64,256]{2,1,0:T(8,128)(2,1)}), bf16[16,64,256]{2,1,0:T(8,128)(2,1)S(1)}, u32[]{:S(2)}, u32[]{:S(2)}) async-start(bf16[16,64,256]{2,1,0:T(8,128)(2,1)} %shard_map.95), calls=%async_computation | async-start | bytes 1048576 | tf_op jit(solution)/shard_map/all_to_all | solution.py:198
  36.5 16.1 %collective-permute-start = (bf16[512,128]{1,0:T(8,128)(2,1)}, bf16[512,128]{1,0:T(8,128)(2,1)S(1)}, u32[]{:S(2)}, u32[]{:S(2)}) collective-permute-start(bf16[512,128]{1,0:T(8,128)(2,1)} %get-tuple-element.22), channel_id=1, source_target_pairs={{0,1},{1,2},{2,3},{3,4},{4,5},{5,6},{6,7},{7,8},{8,9},{9,10},{10,1... | collective-permute-start | bytes 393224 | tf_op jit(solution)/shard_map/ppermute | solution.py:248
  42.9 9.7 %collective-permute-start.1 = (bf16[512,128]{1,0:T(8,128)(2,1)}, bf16[512,128]{1,0:T(8,128)(2,1)S(1)}, u32[]{:S(2)}, u32[]{:S(2)}) collective-permute-start(bf16[512,128]{1,0:T(8,128)(2,1)} %get-tuple-element.23), channel_id=1, source_target_pairs={{1,0},{2,1},{3,2},{4,3},{5,4},{6,5},{7,6},{8,7},{9,8},{10,9},{11,1... | collective-permute-start | bytes 393224 | tf_op jit(solution)/shard_map/ppermute | solution.py:249
  48.0 12.9 %collective-permute-start.10 = (bf16[64,256]{1,0:T(8,128)(2,1)S(1)}, bf16[64,256]{1,0:T(8,128)(2,1)S(1)}, u32[]{:S(2)}, u32[]{:S(2)}) collective-permute-start(bf16[64,256]{1,0:T(8,128)(2,1)S(1)} %shard_map.96.mine_ref), channel_id=1, source_target_pairs={{0,1},{1,0},{2,3},{3,2},{4,5},{5,4},{6,7},{7,6},{8,9},{9,8},{10,11... | collective-permute-start | bytes 98312 | tf_op jit(solution)/shard_map/ppermute | solution.py:273
  65.2 8.8 %collective-permute-start.15 = (bf16[3,128,256]{2,1,0:T(8,128)(2,1)S(1)}, bf16[3,128,256]{2,1,0:T(8,128)(2,1)S(1)}, u32[]{:S(2)}, u32[]{:S(2)}) collective-permute-start(bf16[3,128,256]{2,1,0:T(8,128)(2,1)S(1)} %shard_map.99.refs_0_), channel_id=1, source_target_pairs={{0,4},{2,6},{4,8},{6,10},{8,12},{10,14},{12,0},{14,2},{1,13},{3,15... | collective-permute-start | bytes 589832 | tf_op jit(solution)/shard_map/ppermute | solution.py:244
  69.3 10.0 %collective-permute-start.14 = (bf16[3,128,256]{2,1,0:T(8,128)(2,1)S(1)}, bf16[3,128,256]{2,1,0:T(8,128)(2,1)S(1)}, u32[]{:S(2)}, u32[]{:S(2)}) collective-permute-start(bf16[3,128,256]{2,1,0:T(8,128)(2,1)S(1)} %shard_map.99.refs_0_), channel_id=1, source_target_pairs={{0,2},{2,4},{4,6},{6,8},{8,10},{10,12},{12,14},{14,0},{1,15},{3,1}... | collective-permute-start | bytes 589832 | tf_op jit(solution)/shard_map/ppermute | solution.py:244
  74.0 5.5 %collective-permute-start.16 = (bf16[3,128,256]{2,1,0:T(8,128)(2,1)S(1)}, bf16[3,128,256]{2,1,0:T(8,128)(2,1)S(1)}, u32[]{:S(2)}, u32[]{:S(2)}) collective-permute-start(bf16[3,128,256]{2,1,0:T(8,128)(2,1)S(1)} %collective-permute-done.15.refs_2_), channel_id=1, source_target_pairs={{0,2},{2,4},{4,6},{6,8},{8,10},{10,12},{12,14},{14,0},{1,15},{3,1}... | collective-permute-start | bytes 589832 | tf_op jit(solution)/shard_map/ppermute | solution.py:244
  75.4 6.4 %collective-permute-start.19 = (bf16[3,128,256]{2,1,0:T(8,128)(2,1)S(1)}, bf16[3,128,256]{2,1,0:T(8,128)(2,1)S(1)}, u32[]{:S(2)}, u32[]{:S(2)}) collective-permute-start(bf16[3,128,256]{2,1,0:T(8,128)(2,1)S(1)} %collective-permute-done.15.refs_2_), channel_id=1, source_target_pairs={{0,1},{1,0},{2,3},{3,2},{4,5},{5,4},{6,7},{7,6},{8,9},{9,8},{10,11... | collective-permute-start | bytes 589832 | tf_op jit(solution)/shard_map/ppermute | solution.py:246
  76.9 6.3 %collective-permute-start.17 = (bf16[3,128,256]{2,1,0:T(8,128)(2,1)S(1)}, bf16[3,128,256]{2,1,0:T(8,128)(2,1)S(1)}, u32[]{:S(2)}, u32[]{:S(2)}) collective-permute-start(bf16[3,128,256]{2,1,0:T(8,128)(2,1)S(1)} %collective-permute-done.15.refs_2_), channel_id=1, source_target_pairs={{0,4},{2,6},{4,8},{6,10},{8,12},{10,14},{12,0},{14,2},{1,13},{3,15... | collective-permute-start | bytes 589832 | tf_op jit(solution)/shard_map/ppermute | solution.py:244
  79.3 4.0 %collective-permute-start.18 = (bf16[3,128,256]{2,1,0:T(8,128)(2,1)S(1)}, bf16[3,128,256]{2,1,0:T(8,128)(2,1)S(1)}, u32[]{:S(2)}, u32[]{:S(2)}) collective-permute-start(bf16[3,128,256]{2,1,0:T(8,128)(2,1)S(1)} %collective-permute-done.14.refs_1_), channel_id=1, source_target_pairs={{0,1},{1,0},{2,3},{3,2},{4,5},{5,4},{6,7},{7,6},{8,9},{9,8},{10,11... | collective-permute-start | bytes 589832 | tf_op jit(solution)/shard_map/ppermute | solution.py:246
  79.5 3.8 %collective-permute-start.20 = (bf16[3,128,256]{2,1,0:T(8,128)(2,1)S(1)}, bf16[3,128,256]{2,1,0:T(8,128)(2,1)S(1)}, u32[]{:S(2)}, u32[]{:S(2)}) collective-permute-start(bf16[3,128,256]{2,1,0:T(8,128)(2,1)S(1)} %collective-permute-done.16.refs_3_), channel_id=1, source_target_pairs={{0,1},{1,0},{2,3},{3,2},{4,5},{5,4},{6,7},{7,6},{8,9},{9,8},{10,11... | collective-permute-start | bytes 589832 | tf_op jit(solution)/shard_map/ppermute | solution.py:246
  89.6 14.5 %all-to-all-start.1 = ((bf16[16,64,256]{2,1,0:T(8,128)(2,1)}), bf16[16,64,256]{2,1,0:T(8,128)(2,1)}, u32[]{:S(2)}, u32[]{:S(2)}) async-start(bf16[16,64,256]{2,1,0:T(8,128)(2,1)} %copy-done.12), calls=%async_computation.1 | async-start | bytes 1048576 | tf_op jit(solution)/shard_map/all_to_all | solution.py:198
  95.0 14.8 %collective-permute-start.11 = (bf16[512,128]{1,0:T(8,128)(2,1)}, bf16[512,128]{1,0:T(8,128)(2,1)S(1)}, u32[]{:S(2)}, u32[]{:S(2)}) collective-permute-start(bf16[512,128]{1,0:T(8,128)(2,1)} %copy-done.78), channel_id=1, source_target_pairs={{0,1},{1,2},{2,3},{3,4},{4,5},{5,6},{6,7},{7,8},{8,9},{9,10},{10,1... | collective-permute-start | bytes 393224 | tf_op jit(solution)/shard_map/ppermute | solution.py:248
  99.3 10.6 %collective-permute-start.12 = (bf16[512,128]{1,0:T(8,128)(2,1)}, bf16[512,128]{1,0:T(8,128)(2,1)}, u32[]{:S(2)}, u32[]{:S(2)}) collective-permute-start(bf16[512,128]{1,0:T(8,128)(2,1)} %copy-done.76), channel_id=1, source_target_pairs={{1,0},{2,1},{3,2},{4,3},{5,4},{6,5},{7,6},{8,7},{9,8},{10,9},{11,1... | collective-permute-start | bytes 393224 | tf_op jit(solution)/shard_map/ppermute | solution.py:249
  105.5 13.2 %collective-permute-start.21 = (bf16[64,256]{1,0:T(8,128)(2,1)S(1)}, bf16[64,256]{1,0:T(8,128)(2,1)S(1)}, u32[]{:S(2)}, u32[]{:S(2)}) collective-permute-start(bf16[64,256]{1,0:T(8,128)(2,1)S(1)} %shard_map.102.mine_ref), channel_id=1, source_target_pairs={{0,1},{1,0},{2,3},{3,2},{4,5},{5,4},{6,7},{7,6},{8,9},{9,8},{10,11... | collective-permute-start | bytes 98312 | tf_op jit(solution)/shard_map/ppermute | solution.py:273
  123.1 8.4 %collective-permute-start.26 = (bf16[3,128,256]{2,1,0:T(8,128)(2,1)S(1)}, bf16[3,128,256]{2,1,0:T(8,128)(2,1)S(1)}, u32[]{:S(2)}, u32[]{:S(2)}) collective-permute-start(bf16[3,128,256]{2,1,0:T(8,128)(2,1)S(1)} %shard_map.105.refs_0_), channel_id=1, source_target_pairs={{0,4},{2,6},{4,8},{6,10},{8,12},{10,14},{12,0},{14,2},{1,13},{3,15... | collective-permute-start | bytes 589832 | tf_op jit(solution)/shard_map/ppermute | solution.py:244
  126.7 9.6 %collective-permute-start.25 = (bf16[3,128,256]{2,1,0:T(8,128)(2,1)S(1)}, bf16[3,128,256]{2,1,0:T(8,128)(2,1)S(1)}, u32[]{:S(2)}, u32[]{:S(2)}) collective-permute-start(bf16[3,128,256]{2,1,0:T(8,128)(2,1)S(1)} %shard_map.105.refs_0_), channel_id=1, source_target_pairs={{0,2},{2,4},{4,6},{6,8},{8,10},{10,12},{12,14},{14,0},{1,15},{3,1}... | collective-permute-start | bytes 589832 | tf_op jit(solution)/shard_map/ppermute | solution.py:244
  131.5 5.8 %collective-permute-start.27 = (bf16[3,128,256]{2,1,0:T(8,128)(2,1)S(1)}, bf16[3,128,256]{2,1,0:T(8,128)(2,1)S(1)}, u32[]{:S(2)}, u32[]{:S(2)}) collective-permute-start(bf16[3,128,256]{2,1,0:T(8,128)(2,1)S(1)} %collective-permute-done.26.refs_2_), channel_id=1, source_target_pairs={{0,2},{2,4},{4,6},{6,8},{8,10},{10,12},{12,14},{14,0},{1,15},{3,1}... | collective-permute-start | bytes 589832 | tf_op jit(solution)/shard_map/ppermute | solution.py:244
  133.2 5.7 %collective-permute-start.30 = (bf16[3,128,256]{2,1,0:T(8,128)(2,1)S(1)}, bf16[3,128,256]{2,1,0:T(8,128)(2,1)S(1)}, u32[]{:S(2)}, u32[]{:S(2)}) collective-permute-start(bf16[3,128,256]{2,1,0:T(8,128)(2,1)S(1)} %collective-permute-done.26.refs_2_), channel_id=1, source_target_pairs={{0,1},{1,0},{2,3},{3,2},{4,5},{5,4},{6,7},{7,6},{8,9},{9,8},{10,11... | collective-permute-start | bytes 589832 | tf_op jit(solution)/shard_map/ppermute | solution.py:246
  134.7 5.9 %collective-permute-start.28 = (bf16[3,128,256]{2,1,0:T(8,128)(2,1)S(1)}, bf16[3,128,256]{2,1,0:T(8,128)(2,1)S(1)}, u32[]{:S(2)}, u32[]{:S(2)}) collective-permute-start(bf16[3,128,256]{2,1,0:T(8,128)(2,1)S(1)} %collective-permute-done.26.refs_2_), channel_id=1, source_target_pairs={{0,4},{2,6},{4,8},{6,10},{8,12},{10,14},{12,0},{14,2},{1,13},{3,15... | collective-permute-start | bytes 589832 | tf_op jit(solution)/shard_map/ppermute | solution.py:244
  136.4 4.3 %collective-permute-start.29 = (bf16[3,128,256]{2,1,0:T(8,128)(2,1)S(1)}, bf16[3,128,256]{2,1,0:T(8,128)(2,1)S(1)}, u32[]{:S(2)}, u32[]{:S(2)}) collective-permute-start(bf16[3,128,256]{2,1,0:T(8,128)(2,1)S(1)} %collective-permute-done.25.refs_1_), channel_id=1, source_target_pairs={{0,1},{1,0},{2,3},{3,2},{4,5},{5,4},{6,7},{7,6},{8,9},{9,8},{10,11... | collective-permute-start | bytes 589832 | tf_op jit(solution)/shard_map/ppermute | solution.py:246
  147.0 17.4 %all-to-all-start.2 = ((bf16[16,64,256]{2,1,0:T(8,128)(2,1)}), bf16[16,64,256]{2,1,0:T(8,128)(2,1)}, u32[]{:S(2)}, u32[]{:S(2)}) async-start(bf16[16,64,256]{2,1,0:T(8,128)(2,1)} %copy-done.13), calls=%async_computation.2 | async-start | bytes 1048576 | tf_op jit(solution)/shard_map/all_to_all | solution.py:198
  154.9 14.1 %collective-permute-start.22 = (bf16[512,128]{1,0:T(8,128)(2,1)}, bf16[512,128]{1,0:T(8,128)(2,1)S(1)}, u32[]{:S(2)}, u32[]{:S(2)}) collective-permute-start(bf16[512,128]{1,0:T(8,128)(2,1)} %copy-done.79), channel_id=1, source_target_pairs={{0,1},{1,2},{2,3},{3,4},{4,5},{5,6},{6,7},{7,8},{8,9},{9,10},{10,1... | collective-permute-start | bytes 393224 | tf_op jit(solution)/shard_map/ppermute | solution.py:248
  159.2 9.8 %collective-permute-start.23 = (bf16[512,128]{1,0:T(8,128)(2,1)}, bf16[512,128]{1,0:T(8,128)(2,1)}, u32[]{:S(2)}, u32[]{:S(2)}) collective-permute-start(bf16[512,128]{1,0:T(8,128)(2,1)} %copy-done.77), channel_id=1, source_target_pairs={{1,0},{2,1},{3,2},{4,3},{5,4},{6,5},{7,6},{8,7},{9,8},{10,9},{11,1... | collective-permute-start | bytes 393224 | tf_op jit(solution)/shard_map/ppermute | solution.py:249
  165.8 12.0 %collective-permute-start.32 = (bf16[64,256]{1,0:T(8,128)(2,1)S(1)}, bf16[64,256]{1,0:T(8,128)(2,1)S(1)}, u32[]{:S(2)}, u32[]{:S(2)}) collective-permute-start(bf16[64,256]{1,0:T(8,128)(2,1)S(1)} %shard_map.108.mine_ref), channel_id=1, source_target_pairs={{0,1},{1,0},{2,3},{3,2},{4,5},{5,4},{6,7},{7,6},{8,9},{9,8},{10,11... | collective-permute-start | bytes 98312 | tf_op jit(solution)/shard_map/ppermute | solution.py:273
  (84 other events, 776.0 us)
